TPU v7x, 256 devices: a whole 4x4x8 slice. The times are simulated.
256 devices in a mesh: col: 4 (over y), tile: 64 (over x, z, core).
Axes of the slice: x: 4, y: 4, z: 8, core: 2. Of those that a mesh axis runs over, the one named last changes fastest.
Arguments:
- vectors: float32 [8, 4, 512, 2048], P(None, None, 'tile', 'col'), may hold values from -12 to 12
- onsite: float32 [4, 512, 2048], P(None, 'tile', 'col'), may hold values from -0.3 to 0.3
- intra_hop: float32 [3, 2, 512, 2048], P(None, None, 'tile', 'col'), may hold values from 0.15 to 0.35
- inter_index: int32 [4, 2, 512, 2048], P(None, None, 'tile', 'col'), may hold values from 0 to 18
- inter_hop: float32 [4, 2, 512, 2048], P(None, None, 'tile', 'col'), may hold values from 0.04 to 0.16
Outputs:
- last_term: float32 [8, 4, 512, 2048], P(None, None, 'tile', 'col')
- moments: float32 [7, 8], replicated
Inputs may be any that keep to these rules, and one draw needn't show every extreme that they name: `inter_index`: A code c below 18 names the second-layer orbital of sublattice c // 9 in the cell at offset ((c % 9) // 3 - 1, c % 3 - 1) from the slot's cell; 18 marks an empty slot.
All inputs are finite; a program needn't handle non-finite values.
Results may differ from a plain program's by a relative error of at most 0.000025.
Values sent between devices are 32-bit elements; how exact they have to be, the bound alone decides.
No kernel may reach another device: no remote copies, remote signals or barrier semaphores. Data moves between devices by JAX's collectives and lax.ppermute only.
A program may use at most 64 MiB of HBM per device.

v0:
```python
import jax
import jax.numpy as jnp
from jax import lax
from jax.sharding import Mesh
from jax.sharding import PartitionSpec as P

COL_TILE = ("col", "tile_0", "tile_1", "tile_2")
TILE = ("tile_0", "tile_1", "tile_2")


BOND_OFFSETS = ((0, 0), (-1, 0), (0, -1))


def over_axes(array, axes):
    for axis in axes:
        array = lax.psum(array, axis)
    return array


def extended_2(cells, sides, width):
    for axis, dim in sides:
        count = lax.axis_size(axis)
        head = lax.slice_in_dim(cells, 0, width, axis=dim)
        tail = lax.slice_in_dim(cells, cells.shape[dim] - width, cells.shape[dim], axis=dim)
        cells = jnp.concatenate(
            [
                lax.ppermute(tail, axis, [(i, (i + 1) % count) for i in range(count)]),
                cells,
                lax.ppermute(head, axis, [((i + 1) % count, i) for i in range(count)]),
            ],
            axis=dim,
        )
    return cells


def sliced(array, row_off, col_off):
    rows = array.shape[-2] - 2
    cols = array.shape[-1] - 2
    return array[..., 1 + row_off : 1 + row_off + rows, 1 + col_off : 1 + col_off + cols]


def trim_rim(array, excess):
    return array[..., excess : array.shape[-2] - excess, excess : array.shape[-1] - excess]


def make_weights(neighbours, amplitude):
    return jnp.stack(
        [
            jnp.sum(jnp.where(neighbours == code_no, amplitude, jnp.zeros_like(amplitude)), axis=0)
            for code_no in range(18)
        ],
        axis=1,
    )


def apply_hamiltonian(vector, onsite, intra_hop, weights, pick):
    outputs = []
    for layer_no in range(2):
        side_a = vector[:, 2 * layer_no]
        side_b = vector[:, 2 * layer_no + 1]
        out_a = pick(onsite[2 * layer_no], 0, 0) * pick(side_a, 0, 0)
        out_b = pick(onsite[2 * layer_no + 1], 0, 0) * pick(side_b, 0, 0)
        for bond_idx in range(3):
            row_off, col_off = BOND_OFFSETS[bond_idx]
            out_a = out_a + pick(intra_hop[bond_idx, layer_no], 0, 0) * pick(
                side_b, row_off, col_off
            )
            out_b = out_b + pick(intra_hop[bond_idx, layer_no], -row_off, -col_off) * pick(
                side_a, -row_off, -col_off
            )
        outputs += [out_a, out_b]
    for source in range(2):
        for code_no in range(18):
            target = code_no // 9
            row_off = code_no % 9 // 3 - 1
            col_off = code_no % 3 - 1
            outputs[source] = outputs[source] + pick(weights[source, code_no], 0, 0) * pick(
                vector[:, 2 + target], row_off, col_off
            )
            outputs[2 + target] = outputs[2 + target] + pick(
                weights[source, code_no], -row_off, -col_off
            ) * pick(vector[:, source], -row_off, -col_off)
    return jnp.stack(outputs, axis=1)


def inner_sums(left, right):
    return jnp.sum(left * right, axis=(1, 2, 3))


def moments_from(totals, orbitals):
    scaled = totals / orbitals
    zeroth = scaled[0]
    first = scaled[1]
    return jnp.stack(
        [
            zeroth,
            first,
            2.0 * scaled[2] - zeroth,
            2.0 * scaled[3] - first,
            2.0 * scaled[4] - zeroth,
            2.0 * scaled[5] - first,
            2.0 * scaled[6] - zeroth,
        ]
    )


def reduce_group(group):
    return over_axes(group, COL_TILE)


def on_device(vectors, onsite, intra_hop, inter_index, inter_hop):
    slots = inter_index.shape[0]
    rows = vectors.shape[2]
    cols = vectors.shape[3]
    rim_width = 3
    packed = jnp.concatenate(
        [onsite, intra_hop.reshape(6, rows, cols), inter_hop.reshape(2 * slots, rows, cols)], axis=0
    )
    packed = extended_2(packed, (("col", 2), (TILE, 1)), rim_width)
    codes = extended_2(
        inter_index.reshape(2 * slots, rows, cols), (("col", 2), (TILE, 1)), rim_width
    )
    wide_rows = packed.shape[1]
    wide_cols = packed.shape[2]
    weights = make_weights(
        codes.reshape(slots, 2, wide_rows, wide_cols),
        packed[10:].reshape(slots, 2, wide_rows, wide_cols),
    )

    def operator(extended, margin):
        excess = rim_width - margin
        local_coef = trim_rim(packed, excess)
        return apply_hamiltonian(
            extended,
            local_coef[:4],
            local_coef[4:10].reshape(3, 2, local_coef.shape[1], local_coef.shape[2]),
            trim_rim(weights, excess),
            sliced,
        )

    wide_zero = extended_2(vectors, (("col", 3), (TILE, 2)), 3)
    wide_one = operator(wide_zero, 3)
    wide_two = 2.0 * operator(wide_one, 2) - trim_rim(wide_zero, 2)
    last_term = 2.0 * operator(wide_two, 1) - trim_rim(wide_one, 2)
    term_one = trim_rim(wide_one, 2)
    term_two = trim_rim(wide_two, 1)
    orbitals = 4 * rows * cols * lax.axis_size(TILE) * lax.axis_size("col")
    first_group = reduce_group(
        jnp.stack(
            [
                inner_sums(vectors, vectors),
                inner_sums(term_one, vectors),
                inner_sums(term_one, term_one),
            ]
        )
    )
    second_group = reduce_group(
        jnp.stack([inner_sums(term_two, term_one), inner_sums(term_two, term_two)])
    )
    third_group = reduce_group(
        jnp.stack([inner_sums(last_term, term_two), inner_sums(last_term, last_term)])
    )
    totals = jnp.concatenate([first_group, second_group, third_group], axis=0)
    return (last_term, moments_from(totals, orbitals))


def solution(mesh):
    torus = Mesh(
        mesh.devices.reshape(mesh.shape["col"], 4, 8, 2), ("col", "tile_0", "tile_1", "tile_2")
    )
    placed = (
        P(None, None, TILE, "col"),
        P(None, TILE, "col"),
        P(None, None, TILE, "col"),
        P(None, None, TILE, "col"),
        P(None, None, TILE, "col"),
    )
    return jax.shard_map(
        on_device,
        mesh=torus,
        in_specs=placed,
        out_specs=(P(None, None, TILE, "col"), P()),
        check_vma=False,
    )
```

profile of v0, /device:TPU:1, one launch (start us, length us, event | category | flops | bytes accessed | tf_op | source)
XLA Modules:
  0.0 138.5 jit_solution(3104907049657327457)
XLA Ops:
  0.7 1.1 fusion.1
  1.8 3.6 %collective-permute-start.5 = (f32[8,4,8,3]{3,2,0,1:T(8,128)S(1)}, f32[8,4,8,3]{3,2,0,1:T(8,128)S(1)}, u32[]{:S(2)}, u32[]{:S(2)}) collective-permute-start(f32[8,4,8,3]{3,2,0,1:T(8,128)S(1)} %get-tuple-element.63), channel_id=1, source_target_pairs={{64,0},{128,64},{192,128},{0,192},{65,1},{129,65},{193,129},{1,193... | collective-permute-start | bytes 9224 | tf_op jit(solution)/shard_map/ppermute | solution.py:29
  6.3 2.7 %collective-permute-start.9 = (s32[8,8,3]{2,1,0:T(8,128)S(1)}, s32[8,8,3]{2,1,0:T(8,128)S(1)}, u32[]{:S(2)}, u32[]{:S(2)}) collective-permute-start(s32[8,8,3]{2,1,0:T(8,128)S(1)} %get-tuple-element.89), channel_id=1, source_target_pairs={{64,0},{128,64},{192,128},{0,192},{65,1},{129,65},{193,129},{1,193... | collective-permute-start | bytes 2312 | tf_op jit(solution)/shard_map/ppermute | solution.py:29
  9.9 2.8 %collective-permute-start.1 = (f32[18,8,3]{2,1,0:T(8,128)S(1)}, f32[18,8,3]{2,1,0:T(8,128)S(1)}, u32[]{:S(2)}, u32[]{:S(2)}) collective-permute-start(f32[18,8,3]{2,1,0:T(8,128)S(1)} %get-tuple-element.67), channel_id=1, source_target_pairs={{64,0},{128,64},{192,128},{0,192},{65,1},{129,65},{193,129},{1,193... | collective-permute-start | bytes 5192 | tf_op jit(solution)/shard_map/ppermute | solution.py:29
  12.9 1.0 pad_add_fusion.1
  14.0 2.7 %collective-permute-start.11 = (s32[8,3,518]{2,1,0:T(4,128)S(1)}, s32[8,3,518]{2,1,0:T(4,128)S(1)}, u32[]{:S(2)}, u32[]{:S(2)}) collective-permute-start(s32[8,3,518]{2,1,0:T(4,128)S(1)} %get-tuple-element.87), channel_id=1, source_target_pairs={{1,0},{2,1},{3,2},{4,3},{5,4},{6,5},{7,6},{8,7},{9,8},{10,9},{11,1... | collective-permute-start | bytes 149192 | tf_op jit(solution)/shard_map/ppermute | solution.py:29
  16.7 1.6 %collective-permute-start.10 = (s32[8,3,518]{2,1,0:T(4,128)S(1)}, s32[8,3,518]{2,1,0:T(4,128)S(1)}, u32[]{:S(2)}, u32[]{:S(2)}) collective-permute-start(s32[8,3,518]{2,1,0:T(4,128)S(1)} %get-tuple-element.86), channel_id=1, source_target_pairs={{0,1},{1,2},{2,3},{3,4},{4,5},{5,6},{6,7},{7,8},{8,9},{9,10},{10,1... | collective-permute-start | bytes 149192 | tf_op jit(solution)/shard_map/ppermute | solution.py:27
  18.6 4.0 %collective-permute-start.3 = (f32[18,3,518]{2,1,0:T(4,128)S(1)}, f32[18,3,518]{2,1,0:T(4,128)S(1)}, u32[]{:S(2)}, u32[]{:S(2)}) collective-permute-start(f32[18,3,518]{2,1,0:T(4,128)S(1)} %get-tuple-element.65), channel_id=1, source_target_pairs={{1,0},{2,1},{3,2},{4,3},{5,4},{6,5},{7,6},{8,7},{9,8},{10,9},{11,1... | collective-permute-start | bytes 335672 | tf_op jit(solution)/shard_map/ppermute | solution.py:29
  24.5 5.0 %collective-permute-start.7 = (f32[8,4,3,518]{3,2,0,1:T(4,128)}, f32[8,4,3,518]{3,2,0,1:T(4,128)}, u32[]{:S(2)}, u32[]{:S(2)}) collective-permute-start(f32[8,4,3,518]{3,2,0,1:T(4,128)} %get-tuple-element.61), channel_id=1, source_target_pairs={{1,0},{2,1},{3,2},{4,3},{5,4},{6,5},{7,6},{8,7},{9,8},{10,9},{11,1... | collective-permute-start | bytes 596744 | tf_op jit(solution)/shard_map/ppermute | solution.py:29
  62.5 1.0 reduce_sum.227
  78.4 1.6 %pad_maximum_fusion = f32[8,4,14,518]{3,2,0,1:T(8,128)S(1)} fusion(f32[8,4,3,518]{3,2,0,1:T(4,128)} %collective-permute-done.7, f32[8,4,8,3]{3,2,0,1:T(8,128)S(1)} %copy-done.9, f32[8,4,8,3]{3,2,0,1:T(8,128)S(1)} %copy-done.11, f32[8,4,3,518]{3,2,0,1:T(4,128)} %collective-permute-done.6, f32[8,4,8,512]{3,2,1,0:T(8,128)S(1)} %copy-done.4), kind=kLoop, calls=%fused_computation.1 | loop fusion | flops 928256 | bytes 1856512 | tf_op jit(solution)/shard_map/concatenate | solution.py:25
  80.1 1.5 %multiply_add_fusion = f32[8,12,516]{2,1,0:T(8,128)S(1)} fusion(f32[8,14,518]{2,1,0:T(8,128)S(1)} %get-tuple-element.28, f32[8,14,518]{2,1,0:T(8,128)S(1)} %get-tuple-element.29, f32[8,14,518]{2,1,0:T(8,128)S(1)} %get-tuple-element.27, f32[8,14,518]{2,1,0:T(8,128)S(1)} %get-tuple-element.26, f32[12,516]{1,0:T(8,128)S(1)} %get-tuple-element.419, ...), kind=kLoop, calls=%fused_computation.31 | loop fusion | flops 2130048 | bytes 5102208 | tf_op jit(solution)/shard_map/add | solution.py:80
  81.6 1.6 %multiply_add_fusion.1 = f32[8,12,516]{2,1,0:T(8,128)S(1)} fusion(f32[8,14,518]{2,1,0:T(8,128)S(1)} %get-tuple-element.28, f32[8,14,518]{2,1,0:T(8,128)S(1)} %get-tuple-element.29, f32[8,14,518]{2,1,0:T(8,128)S(1)} %get-tuple-element.26, f32[8,14,518]{2,1,0:T(8,128)S(1)} %get-tuple-element.27, f32[12,516]{1,0:T(8,128)S(1)} %get-tuple-element.435, ...), kind=kLoop, calls=%fused_computation.32 | loop fusion | flops 2130048 | bytes 5102208 | tf_op jit(solution)/shard_map/add | solution.py:80
  83.2 1.4 %multiply_add_fusion.2 = f32[8,12,516]{2,1,0:T(8,128)S(1)} fusion(f32[8,14,518]{2,1,0:T(8,128)S(1)} %get-tuple-element.26, f32[8,14,518]{2,1,0:T(8,128)S(1)} %get-tuple-element.27, f32[8,14,518]{2,1,0:T(8,128)S(1)} %get-tuple-element.29, f32[8,14,518]{2,1,0:T(8,128)S(1)} %get-tuple-element.28, f32[12,516]{1,0:T(8,128)S(1)} %get-tuple-element.420, ...), kind=kLoop, calls=%fused_computation.33 | loop fusion | flops 2130048 | bytes 5102208 | tf_op jit(solution)/shard_map/add | solution.py:77
  84.6 1.4 multiply_add_fusion.3
  86.0 1.5 %add_bitcast_fusion = f32[8,1,10,514]{3,2,0,1:T(8,128)S(1)} fusion(f32[8,12,516]{2,1,0:T(8,128)S(1)} %multiply_add_fusion.2, f32[8,12,516]{2,1,0:T(8,128)S(1)} %multiply_add_fusion.3, f32[8,12,516]{2,1,0:T(8,128)S(1)} %multiply_add_fusion.1, f32[8,12,516]{2,1,0:T(8,128)S(1)} %multiply_add_fusion, f32[10,514]{1,0:T(8,128)S(1)} %get-tuple-element.455, ...), kind=kLoop, calls=%fused_computation.27 | loop fusion | flops 1768160 | bytes 4235360 | tf_op jit(solution)/shard_map/stack | solution.py:83
  87.5 1.4 add_bitcast_fusion.1
  88.8 1.5 %add_bitcast_fusion.2 = f32[8,1,10,514]{3,2,0,1:T(8,128)S(1)} fusion(f32[8,12,516]{2,1,0:T(8,128)S(1)} %multiply_add_fusion, f32[8,12,516]{2,1,0:T(8,128)S(1)} %multiply_add_fusion.1, f32[8,12,516]{2,1,0:T(8,128)S(1)} %multiply_add_fusion.3, f32[8,12,516]{2,1,0:T(8,128)S(1)} %multiply_add_fusion.2, f32[10,514]{1,0:T(8,128)S(1)} %get-tuple-element.456, ...), kind=kLoop, calls=%fused_computation.29 | loop fusion | flops 1768160 | bytes 4235360 | tf_op jit(solution)/shard_map/stack | solution.py:83
  90.3 1.4 add_bitcast_fusion.3
  94.7 1.4 %multiply_reduce_fusion.6 = (f32[8]{0:T(128)S(1)}, f32[8]{0:T(128)S(1)}, f32[8]{0:T(128)S(1)}, f32[8]{0:T(128)S(1)}, f32[8]{0:T(128)S(1)}, /*index=5*/f32[8]{0:T(128)S(1)}, f32[8]{0:T(128)S(1)}, f32[8,4,8,512]{3,2,1,0:T(8,128)}) fusion(f32[8,4,8,512]{3,2,1,0:T(8,128)S(1)} %copy-done.4, f32[8,1,12,516]{3,2,1,0:T(8,128)S(1)} %bitcast.367, ...), kind=kLoop, calls=%fused_computation.16 | loop fusion | flops 2883528 | bytes 3408096 | tf_op jit(solution)/shard_map/reduce_sum | solution.py:87
  96.1 8.4 %all-reduce.2 = (f32[2,8]{1,0:T(2,128)S(1)}, f32[2,8]{1,0:T(2,128)S(1)}, f32[3,8]{1,0:T(4,128)S(1)}) all-reduce(f32[2,8]{1,0:T(2,128)S(1)} %pad_maximum_fusion.12, f32[2,8]{1,0:T(2,128)S(1)} %pad_maximum_fusion.11, f32[3,8]{1,0:T(4,128)S(1)} %pad_maximum_fusion.10), channel_id=1, replica_groups=mesh['col'=4,'tile_0'=4,'tile_1'=8,'tile_2'=2] {'col'}, use_global_device_ids=true, to_apply=%region_33.34 | all-reduce | flops 56 | bytes 448 | tf_op jit(solution)/shard_map/psum | solution.py:16
  104.5 6.0 %all-reduce.1 = (f32[2,8]{1,0:T(2,128)S(1)}, f32[2,8]{1,0:T(2,128)S(1)}, f32[3,8]{1,0:T(4,128)S(1)}) all-reduce(f32[2,8]{1,0:T(2,128)S(1)} %get-tuple-element.15, f32[2,8]{1,0:T(2,128)S(1)} %get-tuple-element.16, f32[3,8]{1,0:T(4,128)S(1)} %get-tuple-element.17), channel_id=1, replica_groups=mesh['col'=4,'tile_0'=4,'tile_1'=8,'tile_2'=2] {'tile_0'}, use_global_device_ids=true, to_apply=%region_34.35 | all-reduce | flops 56 | bytes 448 | tf_op jit(solution)/shard_map/psum | solution.py:16
  110.5 20.6 %all-reduce = (f32[2,8]{1,0:T(2,128)S(1)}, f32[2,8]{1,0:T(2,128)S(1)}, f32[3,8]{1,0:T(4,128)S(1)}) all-reduce(f32[2,8]{1,0:T(2,128)S(1)} %get-tuple-element.12, f32[2,8]{1,0:T(2,128)S(1)} %get-tuple-element.13, f32[3,8]{1,0:T(4,128)S(1)} %get-tuple-element.14), channel_id=1, replica_groups=mesh['col'=4,'tile_0'=4,'tile_1'=8,'tile_2'=2] {'tile_1'}, use_global_device_ids=true, to_apply=%region_35.36 | all-reduce | flops 56 | bytes 448 | tf_op jit(solution)/shard_map/psum | solution.py:16
  131.2 6.7 %all-reduce.3 = (f32[2,8]{1,0:T(2,128)S(1)}, f32[2,8]{1,0:T(2,128)S(1)}, f32[3,8]{1,0:T(4,128)S(1)}) all-reduce(f32[2,8]{1,0:T(2,128)S(1)} %get-tuple-element.9, f32[2,8]{1,0:T(2,128)S(1)} %get-tuple-element.10, f32[3,8]{1,0:T(4,128)S(1)} %get-tuple-element.11), channel_id=1, replica_groups=mesh['col'=4,'tile_0'=4,'tile_1'=8,'tile_2'=2] {'tile_2'}, use_global_device_ids=true, to_apply=%region_36.37 | all-reduce | flops 56 | bytes 448 | tf_op jit(solution)/shard_map/psum | solution.py:16
  (407 shorter events, 53.9 us)
Async XLA Ops:
  0.6 17.7 %copy-start.1 = (f32[4,2,8,512]{3,2,1,0:T(8,128)S(1)}, f32[4,2,8,512]{3,2,1,0:T(8,128)}, u32[]{:S(2)}) copy-start(f32[4,2,8,512]{3,2,1,0:T(8,128)} %param.9) | copy-start | bytes 393220
  0.6 17.7 %copy-start.2 = (f32[3,2,8,512]{3,2,1,0:T(8,128)S(1)}, f32[3,2,8,512]{3,2,1,0:T(8,128)}, u32[]{:S(2)}) copy-start(f32[3,2,8,512]{3,2,1,0:T(8,128)} %param.7) | copy-start | bytes 294916
  0.7 17.7 %copy-start.5 = (f32[4,8,512]{2,1,0:T(8,128)S(1)}, f32[4,8,512]{2,1,0:T(8,128)}, u32[]{:S(2)}) copy-start(f32[4,8,512]{2,1,0:T(8,128)} %param.6) | copy-start | bytes 196612
  1.8 20.8 %collective-permute-start.5 = (f32[8,4,8,3]{3,2,0,1:T(8,128)S(1)}, f32[8,4,8,3]{3,2,0,1:T(8,128)S(1)}, u32[]{:S(2)}, u32[]{:S(2)}) collective-permute-start(f32[8,4,8,3]{3,2,0,1:T(8,128)S(1)} %get-tuple-element.63), channel_id=1, source_target_pairs={{64,0},{128,64},{192,128},{0,192},{65,1},{129,65},{193,129},{1,193... | collective-permute-start | bytes 9224 | tf_op jit(solution)/shard_map/ppermute | solution.py:29
  5.4 17.2 %collective-permute-start.4 = (f32[8,4,8,3]{3,2,0,1:T(8,128)S(1)}, f32[8,4,8,3]{3,2,0,1:T(8,128)S(1)}, u32[]{:S(2)}, u32[]{:S(2)}) collective-permute-start(f32[8,4,8,3]{3,2,0,1:T(8,128)S(1)} %get-tuple-element.62), channel_id=1, source_target_pairs={{0,64},{64,128},{128,192},{192,0},{1,65},{65,129},{129,193},{193,1... | collective-permute-start | bytes 9224 | tf_op jit(solution)/shard_map/ppermute | solution.py:27
  6.3 6.4 %collective-permute-start.9 = (s32[8,8,3]{2,1,0:T(8,128)S(1)}, s32[8,8,3]{2,1,0:T(8,128)S(1)}, u32[]{:S(2)}, u32[]{:S(2)}) collective-permute-start(s32[8,8,3]{2,1,0:T(8,128)S(1)} %get-tuple-element.89), channel_id=1, source_target_pairs={{64,0},{128,64},{192,128},{0,192},{65,1},{129,65},{193,129},{1,193... | collective-permute-start | bytes 2312 | tf_op jit(solution)/shard_map/ppermute | solution.py:29
  9.0 4.0 %collective-permute-start.8 = (s32[8,8,3]{2,1,0:T(8,128)S(1)}, s32[8,8,3]{2,1,0:T(8,128)S(1)}, u32[]{:S(2)}, u32[]{:S(2)}) collective-permute-start(s32[8,8,3]{2,1,0:T(8,128)S(1)} %get-tuple-element.88), channel_id=1, source_target_pairs={{0,64},{64,128},{128,192},{192,0},{1,65},{65,129},{129,193},{193,1... | collective-permute-start | bytes 2312 | tf_op jit(solution)/shard_map/ppermute | solution.py:27
  9.0 14.4 %copy-start.4 = (f32[8,4,8,512]{3,2,1,0:T(8,128)S(1)}, f32[8,4,8,512]{3,2,1,0:T(8,128)}, u32[]{:S(2)}) copy-start(f32[8,4,8,512]{3,2,1,0:T(8,128)} %param.5) | copy-start | bytes 1572868
  9.9 6.8 %collective-permute-start.1 = (f32[18,8,3]{2,1,0:T(8,128)S(1)}, f32[18,8,3]{2,1,0:T(8,128)S(1)}, u32[]{:S(2)}, u32[]{:S(2)}) collective-permute-start(f32[18,8,3]{2,1,0:T(8,128)S(1)} %get-tuple-element.67), channel_id=1, source_target_pairs={{64,0},{128,64},{192,128},{0,192},{65,1},{129,65},{193,129},{1,193... | collective-permute-start | bytes 5192 | tf_op jit(solution)/shard_map/ppermute | solution.py:29
  12.7 5.7 %collective-permute-start = (f32[18,8,3]{2,1,0:T(8,128)S(1)}, f32[18,8,3]{2,1,0:T(8,128)S(1)}, u32[]{:S(2)}, u32[]{:S(2)}) collective-permute-start(f32[18,8,3]{2,1,0:T(8,128)S(1)} %get-tuple-element.66), channel_id=1, source_target_pairs={{0,64},{64,128},{128,192},{192,0},{1,65},{65,129},{129,193},{193,1... | collective-permute-start | bytes 5192 | tf_op jit(solution)/shard_map/ppermute | solution.py:27
  14.0 16.9 %collective-permute-start.11 = (s32[8,3,518]{2,1,0:T(4,128)S(1)}, s32[8,3,518]{2,1,0:T(4,128)S(1)}, u32[]{:S(2)}, u32[]{:S(2)}) collective-permute-start(s32[8,3,518]{2,1,0:T(4,128)S(1)} %get-tuple-element.87), channel_id=1, source_target_pairs={{1,0},{2,1},{3,2},{4,3},{5,4},{6,5},{7,6},{8,7},{9,8},{10,9},{11,1... | collective-permute-start | bytes 149192 | tf_op jit(solution)/shard_map/ppermute | solution.py:29
  16.7 14.2 %collective-permute-start.10 = (s32[8,3,518]{2,1,0:T(4,128)S(1)}, s32[8,3,518]{2,1,0:T(4,128)S(1)}, u32[]{:S(2)}, u32[]{:S(2)}) collective-permute-start(s32[8,3,518]{2,1,0:T(4,128)S(1)} %get-tuple-element.86), channel_id=1, source_target_pairs={{0,1},{1,2},{2,3},{3,4},{4,5},{5,6},{6,7},{7,8},{8,9},{9,10},{10,1... | collective-permute-start | bytes 149192 | tf_op jit(solution)/shard_map/ppermute | solution.py:27
  18.6 11.0 %collective-permute-start.3 = (f32[18,3,518]{2,1,0:T(4,128)S(1)}, f32[18,3,518]{2,1,0:T(4,128)S(1)}, u32[]{:S(2)}, u32[]{:S(2)}) collective-permute-start(f32[18,3,518]{2,1,0:T(4,128)S(1)} %get-tuple-element.65), channel_id=1, source_target_pairs={{1,0},{2,1},{3,2},{4,3},{5,4},{6,5},{7,6},{8,7},{9,8},{10,9},{11,1... | collective-permute-start | bytes 335672 | tf_op jit(solution)/shard_map/ppermute | solution.py:29
  22.6 7.0 %collective-permute-start.2 = (f32[18,3,518]{2,1,0:T(4,128)S(1)}, f32[18,3,518]{2,1,0:T(4,128)S(1)}, u32[]{:S(2)}, u32[]{:S(2)}) collective-permute-start(f32[18,3,518]{2,1,0:T(4,128)S(1)} %get-tuple-element.64), channel_id=1, source_target_pairs={{0,1},{1,2},{2,3},{3,4},{4,5},{5,6},{6,7},{7,8},{8,9},{9,10},{10,1... | collective-permute-start | bytes 335672 | tf_op jit(solution)/shard_map/ppermute | solution.py:27
  24.5 6.4 %copy-start.3 = (s32[4,2,8,512]{3,2,1,0:T(8,128)S(1)}, s32[4,2,8,512]{3,2,1,0:T(8,128)}, u32[]{:S(2)}) copy-start(s32[4,2,8,512]{3,2,1,0:T(8,128)} %param.8) | copy-start | bytes 393220
  24.5 53.8 %collective-permute-start.7 = (f32[8,4,3,518]{3,2,0,1:T(4,128)}, f32[8,4,3,518]{3,2,0,1:T(4,128)}, u32[]{:S(2)}, u32[]{:S(2)}) collective-permute-start(f32[8,4,3,518]{3,2,0,1:T(4,128)} %get-tuple-element.61), channel_id=1, source_target_pairs={{1,0},{2,1},{3,2},{4,3},{5,4},{6,5},{7,6},{8,7},{9,8},{10,9},{11,1... | collective-permute-start | bytes 596744 | tf_op jit(solution)/shard_map/ppermute | solution.py:29
  29.6 48.8 %collective-permute-start.6 = (f32[8,4,3,518]{3,2,0,1:T(4,128)}, f32[8,4,3,518]{3,2,0,1:T(4,128)}, u32[]{:S(2)}, u32[]{:S(2)}) collective-permute-start(f32[8,4,3,518]{3,2,0,1:T(4,128)} %get-tuple-element.60), channel_id=1, source_target_pairs={{0,1},{1,2},{2,3},{3,4},{4,5},{5,6},{6,7},{7,8},{8,9},{9,10},{10,1... | collective-permute-start | bytes 596744 | tf_op jit(solution)/shard_map/ppermute | solution.py:27
  29.9 31.7 %copy-start = (f32[18,14,518]{2,1,0:T(8,128)}, f32[18,14,518]{2,1,0:T(8,128)S(1)}, u32[]{:S(2)}) copy-start(f32[18,14,518]{2,1,0:T(8,128)S(1)} %pad_maximum_fusion.1) | copy-start | bytes 1566436
  68.7 2.9 %copy-start.39 = (f32[14,518]{1,0:T(8,128)S(1)}, f32[14,518]{1,0:T(8,128)}, u32[]{:S(2)}) copy-start(f32[14,518]{1,0:T(8,128)} %get-tuple-element.192) | copy-start | bytes 87028
  68.7 2.9 %copy-start.40 = (f32[14,518]{1,0:T(8,128)S(1)}, f32[14,518]{1,0:T(8,128)}, u32[]{:S(2)}) copy-start(f32[14,518]{1,0:T(8,128)} %get-tuple-element.193) | copy-start | bytes 87028
  68.9 2.9 %copy-start.41 = (f32[14,518]{1,0:T(8,128)S(1)}, f32[14,518]{1,0:T(8,128)}, u32[]{:S(2)}) copy-start(f32[14,518]{1,0:T(8,128)} %get-tuple-element.190) | copy-start | bytes 87028
  68.9 2.9 %copy-start.42 = (f32[14,518]{1,0:T(8,128)S(1)}, f32[14,518]{1,0:T(8,128)}, u32[]{:S(2)}) copy-start(f32[14,518]{1,0:T(8,128)} %get-tuple-element.191) | copy-start | bytes 87028
  68.9 3.0 %copy-start.43 = (f32[14,518]{1,0:T(8,128)S(1)}, f32[14,518]{1,0:T(8,128)}, u32[]{:S(2)}) copy-start(f32[14,518]{1,0:T(8,128)} %get-tuple-element.188) | copy-start | bytes 87028
  68.9 3.0 %copy-start.44 = (f32[14,518]{1,0:T(8,128)S(1)}, f32[14,518]{1,0:T(8,128)}, u32[]{:S(2)}) copy-start(f32[14,518]{1,0:T(8,128)} %get-tuple-element.189) | copy-start | bytes 87028
  (86 other events, 118.5 us)
where the time goes:
time: 139 us; the launch traced here: 138 us
  local copies, waits for them, and re-layouts  47.2 us (34%)
  blocking collectives  41.7 us (30%)
  other arithmetic  24 us (17%)
  starting transfers between devices  22.5 us (16%)
  between operations  2.8 us (2%)
    psum x4, blocking collectives, over_axes(): array = lax.psum(array, axis)  41.7 us
    squeeze x54, local copies, waits for them, and re-layouts, apply_hamiltonian(): weights[source, code_no]  31.1 us
    ppermute x6, starting transfers between devices, extended_2(): lax.ppermute(head, axis, [((i + 1) % count, i) for i in range(count)])  20.8 us
    slice x84, local copies, waits for them, and re-layouts, sliced(): array[..., 1 + row_off:1 + row_off + rows, 1 + col_off:1 + col_off + cols]  9.12 us
    another operation x8, other arithmetic, apply_hamiltonian(): return jnp.stack(outputs, axis=1)  8.09 us
    concatenate x5, other arithmetic, extended_2(): jnp.concatenate([lax.ppermute(tail, axis, [(i, (i + 1) % count) for i in...  3.38 us
    add x2, other arithmetic, apply_hamiltonian(): outputs[2 + target]  3.05 us
    slice x5, local copies, waits for them, and re-layouts, extended_2(): lax.slice_in_dim(cells, cells.shape[dim] - width, cells.shape[dim], axis=...  2.98 us
  transfers between devices with their start and end apart: 12, of which 1 were waited for; matrix products, arithmetic and copies ran while one was open for 37% of the time, Pallas kernels for 0%

commit v1 on v0

v1 whole, which is shorter than its diff:
```python
import functools

import jax
import jax.numpy as jnp
from jax import lax
from jax.experimental import pallas as pl
from jax.experimental.pallas import tpu as pltpu
from jax.sharding import Mesh
from jax.sharding import PartitionSpec as P

TILE = ("tile_0", "tile_1", "tile_2")
EVERY = ("col",) + TILE

V = 8
R = 8
C = 512
W = C + 128
RING = 16
RIM = 3
COEFS = 26
LANES = 128
FIELD_ROWS = 4 * RIM * V
ROW_MSG = FIELD_ROWS + COEFS * 4

FWD = 0
SHIFTED = 36
INTRA = 60
INTRA_SHIFTED = 66
ONSITE = 68
PLANES = 72

SIDE_CODES = [code for code in range(18) if code % 3 != 1]


def offsets(code):
    return code % 9 // 3 - 1, code % 3 - 1


def shifted_plane(source, code):
    if code % 3 == 1:
        return FWD + source * 18 + code
    return SHIFTED + source * 12 + SIDE_CODES.index(code)


def lanes_of(shape):
    return lax.broadcasted_iota(jnp.int32, shape, len(shape) - 1)


def subs_of(shape):
    return lax.broadcasted_iota(jnp.int32, shape, len(shape) - 2)


def lane_roll(array, amount):
    amount = amount % array.shape[-1]
    if amount == 0:
        return array
    return pltpu.roll(array, amount, axis=array.ndim - 1)


def pack_kernel(vec, onsite, intra, codes, inter, field, up_msg, down_msg, left_msg, right_msg):
    for orbital in range(4):
        for block in range(C // LANES):
            cols = slice(block * LANES, (block + 1) * LANES)
            turned = jnp.swapaxes(vec[:, orbital, :, cols], 0, 1)
            for row in range(R):
                field[pl.ds((orbital * R + row) * V, V), cols] = turned[row]
                if row < RIM:
                    up_msg[pl.ds((orbital * RIM + row) * V, V), cols] = turned[row]
                if row >= R - RIM:
                    at = row - (R - RIM)
                    down_msg[pl.ds((orbital * RIM + at) * V, V), cols] = turned[row]

    def plane(index):
        if index < 4:
            return onsite[index]
        if index < 10:
            return intra[(index - 4) // 2, (index - 4) % 2]
        if index < 18:
            return codes[(index - 10) // 2, (index - 10) % 2].astype(jnp.float32)
        return inter[(index - 18) // 2, (index - 18) % 2]

    low = subs_of((R, C)) < 4
    for pair in range(COEFS // 2):
        even, odd = plane(2 * pair), plane(2 * pair + 1)
        odd_turned = pltpu.roll(odd, 4, axis=0)
        rows = pl.ds(FIELD_ROWS + pair * R, R)
        up_msg[rows, :] = jnp.where(low, even, odd_turned)
        down_msg[rows, :] = jnp.where(low, odd_turned, even)

    lane = lanes_of((R, LANES))
    left = jnp.zeros((R, LANES), jnp.float32)
    right = jnp.zeros((R, LANES), jnp.float32)
    for slot in range(32):
        rows = pl.ds(slot * V, V)
        inside = (lane >= 4 * slot) & (lane < 4 * slot + 4)
        left = jnp.where(inside, lane_roll(field[rows, 0:LANES], 4 * slot), left)
        right = jnp.where(inside, lane_roll(field[rows, C - LANES : C], 4 * slot + 4), right)
    left_msg[0:8, :] = left
    right_msg[0:8, :] = right
    left = jnp.zeros((R, LANES), jnp.float32)
    right = jnp.zeros((R, LANES), jnp.float32)
    for slot in range(COEFS):
        values = plane(slot)
        inside = (lane >= 4 * slot) & (lane < 4 * slot + 4)
        left = jnp.where(inside, lane_roll(values[:, 0:LANES], 4 * slot), left)
        right = jnp.where(inside, lane_roll(values[:, C - LANES : C], 4 * slot + 4), right)
    left_msg[8:16, :] = left
    right_msg[8:16, :] = right


def pack(vectors, onsite, intra, codes, inter):
    f32 = jnp.float32
    return pl.pallas_call(
        pack_kernel,
        out_shape=(
            jax.ShapeDtypeStruct((4 * R * V, C), f32),
            jax.ShapeDtypeStruct((ROW_MSG, C), f32),
            jax.ShapeDtypeStruct((ROW_MSG, C), f32),
            jax.ShapeDtypeStruct((16, LANES), f32),
            jax.ShapeDtypeStruct((16, LANES), f32),
        ),
        name="pack",
    )(vectors, onsite, intra, codes, inter)


def table_rows(plane, block, half):
    return pl.ds((block * PLANES + plane) * RING + half * R, R)


def shift_plane(table, source, target, half, amount):
    blocks = range(W // LANES)
    row = jnp.concatenate([table[table_rows(source, block, half), :] for block in blocks], axis=1)
    row = lane_roll(row, amount)
    for block in blocks:
        table[table_rows(target, block, half), :] = row[:, block * LANES : (block + 1) * LANES]


def build_table(onsite, intra, codes, inter, below, above, edge_left, edge_right, table):
    low = subs_of((R, LANES)) < 4
    lane = lanes_of((R, LANES))

    def plane_tile(index, block, half):
        cols = slice(block * LANES, (block + 1) * LANES)
        if block == C // LANES:
            return jnp.where(
                lane < 64,
                lane_roll(edge_right[half], -4 * index),
                lane_roll(edge_left[half], 124 - 4 * index),
            )
        if half == 0:
            if index < 4:
                return onsite[index, :, cols]
            if index < 10:
                return intra[(index - 4) // 2, (index - 4) % 2, :, cols]
            if index < 18:
                return codes[(index - 10) // 2, (index - 10) % 2, :, cols].astype(jnp.float32)
            return inter[(index - 18) // 2, (index - 18) % 2, :, cols]
        rows = pl.ds(FIELD_ROWS + index // 2 * R, R)
        if index % 2 == 0:
            return jnp.where(low, below[rows, cols], above[rows, cols])
        return pltpu.roll(jnp.where(low, above[rows, cols], below[rows, cols]), 4, axis=0)

    for half in range(2):
        def put(plane, block, values):
            table[table_rows(plane, block, half), :] = values

        for block in range(W // LANES):
            for index in range(4):
                put(ONSITE + index, block, 2.0 * plane_tile(index, block, half))
            for index in range(6):
                put(INTRA + index, block, 2.0 * plane_tile(4 + index, block, half))
            for source in range(2):
                marks = [plane_tile(10 + 2 * k + source, block, half) for k in range(4)]
                hops = [2.0 * plane_tile(18 + 2 * k + source, block, half) for k in range(4)]
                for code in range(18):
                    terms = [jnp.where(m == float(code), h, 0.0) for m, h in zip(marks, hops)]
                    put(
                        FWD + source * 18 + code,
                        block,
                        (terms[0] + terms[1]) + (terms[2] + terms[3]),
                    )
        for source in range(2):
            for code in SIDE_CODES:
                shift_plane(
                    table,
                    FWD + source * 18 + code,
                    shifted_plane(source, code),
                    half,
                    offsets(code)[1],
                )
        for layer in range(2):
            shift_plane(table, INTRA + 4 + layer, INTRA_SHIFTED + layer, half, -1)


def field_rows(orbital, row):
    start = (orbital * RING + row) * V
    if not isinstance(start, int):
        start = pl.multiple_of(start, V)
    return pl.ds(start, V)


def put_row(field, orbital, row, values):
    rows = field_rows(orbital, row)
    field[1, rows, :] = values
    field[0, rows, :] = lane_roll(values, 1)
    field[2, rows, :] = lane_roll(values, -1)


def stencil_cell(field, table, row, block):
    cols = slice(block * LANES, (block + 1) * LANES)
    at = [(row - 1) & (RING - 1), row, (row + 1) & (RING - 1)]
    cache = {}

    def value(orbital, row_off, col_off):
        key = (orbital, row_off, col_off)
        if key not in cache:
            cache[key] = field[1 + col_off, field_rows(orbital, at[1 + row_off]), cols]
        return cache[key]

    def coef(plane, row_off):
        return table[pl.ds((block * PLANES + plane) * RING + at[1 + row_off], V, stride=0), :]

    sums = [[None, None] for _ in range(4)]

    def add(orbital, term):
        pair = sums[orbital]
        turn = counts[orbital] % 2
        pair[turn] = term if pair[turn] is None else pair[turn] + term
        counts[orbital] += 1

    counts = [0, 0, 0, 0]
    for layer in range(2):
        a, b = 2 * layer, 2 * layer + 1
        add(a, coef(ONSITE + a, 0) * value(a, 0, 0))
        add(b, coef(ONSITE + b, 0) * value(b, 0, 0))
        straight = coef(INTRA + layer, 0)
        add(a, straight * value(b, 0, 0))
        add(b, straight * value(a, 0, 0))
        add(a, coef(INTRA + 2 + layer, 0) * value(b, -1, 0))
        add(b, coef(INTRA + 2 + layer, 1) * value(a, 1, 0))
        add(a, coef(INTRA + 4 + layer, 0) * value(b, 0, -1))
        add(b, coef(INTRA_SHIFTED + layer, 0) * value(a, 0, 1))
    for code in range(18):
        target = 2 + code // 9
        row_off, col_off = offsets(code)
        for source in range(2):
            add(source, coef(FWD + source * 18 + code, 0) * value(target, row_off, col_off))
            add(
                target,
                coef(shifted_plane(source, code), -row_off) * value(source, -row_off, -col_off),
            )
    return [pair[0] + pair[1] for pair in sums]


def moments_kernel_body(
    first, onsite, intra, codes, inter, below, above, left, right, below_corner, above_corner,
    out, partial, zero, one, two, table, last
):
    blocks = C // LANES
    low = subs_of((R, LANES)) < 4
    lane = lanes_of((R, LANES))
    edge_left = [
        left[8:16, :],
        jnp.where(low, below_corner[8:16, :], above_corner[8:16, :]),
    ]
    edge_right = [
        right[8:16, :],
        jnp.where(low, below_corner[24:32, :], above_corner[24:32, :]),
    ]
    build_table(onsite, intra, codes, inter, below, above, edge_left, edge_right, table)

    for orbital in range(4):
        for row in list(range(R + RIM)) + list(range(RING - RIM, RING)):
            if row < R:
                middle = first[pl.ds((orbital * R + row) * V, V), :]
                sides = (left[0:8, :], right[0:8, :])
            elif row < R + RIM:
                middle = below[pl.ds((orbital * RIM + row - R) * V, V), :]
                sides = (below_corner[0:8, :], below_corner[16:24, :])
            else:
                middle = above[pl.ds((orbital * RIM + row - (RING - RIM)) * V, V), :]
                sides = (above_corner[0:8, :], above_corner[16:24, :])
            slot = orbital * 8 + row % 8
            rim = jnp.where(
                lane < 64, lane_roll(sides[1], -4 * slot), lane_roll(sides[0], 124 - 4 * slot)
            )
            put_row(zero, orbital, row, jnp.concatenate([middle, rim], axis=1))

    def first_row(step, carry):
        row = (step - 2) & (RING - 1)
        results = [stencil_cell(zero, table, row, block) for block in range(W // LANES)]
        for orbital in range(4):
            values = jnp.concatenate([0.5 * r[orbital] for r in results], axis=1)
            put_row(one, orbital, row, values)
        return carry

    lax.fori_loop(0, R + 4, first_row, 0)

    def second_row(step, carry):
        row = (step - 1) & (RING - 1)
        results = [stencil_cell(one, table, row, block) for block in range(W // LANES)]
        for orbital in range(4):
            values = jnp.concatenate([r[orbital] for r in results], axis=1)
            values = values - zero[1, field_rows(orbital, row), :]
            put_row(two, orbital, row, values)
        return carry

    lax.fori_loop(0, R + 2, second_row, 0)

    def third_row(row, sums):
        sums = list(sums)
        for block in range(blocks):
            cols = slice(block * LANES, (block + 1) * LANES)
            result = stencil_cell(two, table, row, block)
            for orbital in range(4):
                rows = field_rows(orbital, row)
                t0 = zero[1, rows, cols]
                t1 = one[1, rows, cols]
                t2 = two[1, rows, cols]
                t3 = result[orbital] - t1
                last[pl.ds(pl.multiple_of((orbital * R + row) * V, V), V), cols] = t3
                for at, (x, y) in enumerate(
                    ((t0, t0), (t1, t0), (t1, t1), (t2, t1), (t2, t2), (t3, t2), (t3, t3))
                ):
                    sums[at] = sums[at] + x * y
        return tuple(sums)

    empty = jnp.zeros((V, LANES), jnp.float32)
    sums = lax.fori_loop(0, R, third_row, (empty,) * 7)

    for orbital in range(4):
        for block in range(blocks):
            cols = slice(block * LANES, (block + 1) * LANES)
            rows = pl.ds(orbital * R * V, R * V)
            turned = jnp.swapaxes(last[rows, cols].reshape(R, V, LANES), 0, 1)
            out[:, orbital, :, cols] = turned

    spread = empty
    sub = subs_of((V, LANES))
    for at in range(7):
        total = jnp.sum(sums[at], axis=1, keepdims=True)
        spread = jnp.where(lane == 8 * at + sub, total, spread)
    line = jnp.sum(spread, axis=0, keepdims=True)
    partial[...] = jnp.broadcast_to(line, partial.shape)


def apply_terms(devices, *args):
    f32 = jnp.float32
    return pl.pallas_call(
        moments_kernel_body,
        out_shape=(
            jax.ShapeDtypeStruct((V, 4, R, C), f32),
            jax.ShapeDtypeStruct((devices, LANES), f32),
        ),
        scratch_shapes=[
            pltpu.VMEM((3, 4 * RING * V, W), f32),
            pltpu.VMEM((3, 4 * RING * V, W), f32),
            pltpu.VMEM((3, 4 * RING * V, W), f32),
            pltpu.VMEM((W // LANES * PLANES * RING, LANES), f32),
            pltpu.VMEM((4 * R * V, C), f32),
        ],
        name="terms",
    )(*args)


def finish_kernel(orbitals, parts, out):
    line = jnp.sum(parts[...], axis=0, keepdims=True) / orbitals
    rows = [lane_roll(line, -8 * at)[:, 0:V] for at in range(7)]
    out[0:1, :] = rows[0]
    out[1:2, :] = rows[1]
    for at in range(2, 7):
        out[at : at + 1, :] = 2.0 * rows[at] - rows[at % 2]


def finish(parts, orbitals):
    return pl.pallas_call(
        functools.partial(finish_kernel, orbitals),
        out_shape=jax.ShapeDtypeStruct((7, V), jnp.float32),
        name="finish",
    )(parts)


def on_device(vectors, onsite, intra_hop, inter_index, inter_hop):
    cols = lax.axis_size("col")
    tiles = lax.axis_size(TILE)
    devices = cols * tiles

    def ring(count, step):
        return [(i, (i + step) % count) for i in range(count)]

    field, up_msg, down_msg, left_msg, right_msg = pack(
        vectors, onsite, intra_hop, inter_index, inter_hop
    )
    below = lax.ppermute(up_msg, TILE, ring(tiles, -1))
    above = lax.ppermute(down_msg, TILE, ring(tiles, 1))
    right = lax.ppermute(left_msg, "col", ring(cols, -1))
    left = lax.ppermute(right_msg, "col", ring(cols, 1))
    corner = jnp.concatenate([left, right], axis=0)
    below_corner = lax.ppermute(corner, TILE, ring(tiles, -1))
    above_corner = lax.ppermute(corner, TILE, ring(tiles, 1))
    last_term, partial = apply_terms(
        devices, field, onsite, intra_hop, inter_index, inter_hop,
        below, above, left, right, below_corner, above_corner,
    )
    parts = lax.all_to_all(partial, EVERY, 0, 0)
    return last_term, finish(parts, 4.0 * R * C * devices)


def solution(mesh):
    torus = Mesh(
        mesh.devices.reshape(mesh.shape["col"], 4, 8, 2), ("col", "tile_0", "tile_1", "tile_2")
    )
    placed = (
        P(None, None, TILE, "col"),
        P(None, TILE, "col"),
        P(None, None, TILE, "col"),
        P(None, None, TILE, "col"),
        P(None, None, TILE, "col"),
    )
    return jax.shard_map(
        on_device,
        mesh=torus,
        in_specs=placed,
        out_specs=(P(None, None, TILE, "col"), P()),
        check_vma=False,
    )
```

time: 139 us -> 66.5 us (0.48)
  local copies, waits for them, and re-layouts: 47.2 us -> 2.07 us
  other arithmetic: 24 us -> 0 us
  Pallas kernels: 0 us -> 20.3 us
  blocking collectives: 41.7 us -> 28.4 us
  starting transfers between devices: 22.5 us -> 12.8 us
  between operations: 2.8 us -> 0.65 us
  waiting for transfers between devices: 0.3 us -> 2.09 us
    psum x4 -> x0, blocking collectives: 41.7 us -> none  [over_axes(): array = lax.psum(array, axis)]
    squeeze x59 -> x0, local copies, waits for them, and re-layouts: 31.4 us -> none  [the longest x54 31.1 us: apply_hamiltonian(): weights[source, code_no]]
    all_to_all x0 -> x1, blocking collectives: none -> 28.4 us  [on_device(): parts = lax.all_to_all(partial, EVERY, 0, 0)]
    pallas_call x0 -> x3, Pallas kernels: none -> 20.3 us  [the longest x1 16.2 us: apply_terms(): pl.pallas_call(moments_kernel_body, out_shape=(jax.ShapeDtypeStruct((V, 4...]
    slice x94 -> x0, local copies, waits for them, and re-layouts: 13.9 us -> none  [the longest x84 9.12 us: sliced(): array[..., 1 + row_off:1 + row_off + rows, 1 + col_off:1 + col_off + cols]]
    ppermute x12 -> x6, starting transfers between devices: 22.5 us -> 12.8 us  [the longest x1 5.46 us: on_device(): below_corner = lax.ppermute(corner, TILE, ring(tiles, -1))]
    another operation x11 -> x0, other arithmetic: 8.12 us -> none  [the longest x8 8.09 us: apply_hamiltonian(): return jnp.stack(outputs, axis=1)]
    add x4 -> x0, other arithmetic: 5.87 us -> none  [the longest x2 3.05 us: apply_hamiltonian(): outputs[2 + target]]
  transfers between devices with their start and end apart: 12 -> 6, of which waited for: 1 -> 3; matrix products, arithmetic and copies ran while one was open for 37% -> 0% of each run, Pallas kernels for 0% -> 0%
where the time goes in v1:
time: 66.5 us; the launch traced here: 66.3 us
  blocking collectives  28.4 us (43%)
  Pallas kernels  20.3 us (31%)
  starting transfers between devices  12.8 us (19%)
  waiting for transfers between devices  2.09 us (3%)
  local copies, waits for them, and re-layouts  2.07 us (3%)
    all_to_all x1, blocking collectives, on_device(): parts = lax.all_to_all(partial, EVERY, 0, 0)  28.4 us
    pallas_call x1, Pallas kernels, apply_terms(): pl.pallas_call(moments_kernel_body, out_shape=(jax.ShapeDtypeStruct((V, 4...  16.2 us
    ppermute x1, starting transfers between devices, on_device(): below_corner = lax.ppermute(corner, TILE, ring(tiles, -1))  5.46 us
    ppermute x1, starting transfers between devices, on_device(): below = lax.ppermute(up_msg, TILE, ring(tiles, -1))  3.2 us
    pallas_call x1, Pallas kernels, pack(): pl.pallas_call(pack_kernel, out_shape=(jax.ShapeDtypeStruct((4 * R * V, C...  2.47 us
    unnamed x13, local copies, waits for them, and re-layouts  2.06 us
    pallas_call x1, Pallas kernels, finish(): pl.pallas_call(functools.partial(finish_kernel, orbitals), out_shape=jax....  1.61 us
    ppermute x1, starting transfers between devices, on_device(): right = lax.ppermute(left_msg, 'col', ring(cols, -1))  1.56 us
  transfers between devices with their start and end apart: 6, of which 3 were waited for; matrix products, arithmetic and copies ran while one was open for 0% of the time, Pallas kernels for 0%

profile of v1, /device:TPU:1, one launch (start us, length us, event | category | flops | bytes accessed | tf_op | source)
XLA Modules:
  0.0 66.3 jit_solution(6913334529755612944)
XLA Ops:
  0.6 2.5 %pack.1 = (f32[256,512]{1,0:T(8,128)}, f32[200,512]{1,0:T(8,128)}, f32[200,512]{1,0:T(8,128)}, f32[16,128]{1,0:T(8,128)}, f32[16,128]{1,0:T(8,128)}) custom-call(f32[8,4,8,512]{3,2,1,0:T(8,128)} %vec.1, f32[4,8,512]{2,1,0:T(8,128)} %onsite.3, f32[3,2,8,512]{3,2,1,0:T(8,128)} %intra.3, s32[4,2,8,512]{3,2,1,0:T(8,128)} %codes.3, f32[4,2,8,512]{3,2,1,0:T(8,128)} %inter.3), custom_call_target="tpu_custom_call" | custom-call | tf_op jit(solution)/shard_map/pack/pallas_call | solution.py:113
  3.1 3.2 %collective-permute-start = (f32[200,512]{1,0:T(8,128)}, f32[200,512]{1,0:T(8,128)S(1)}, u32[]{:S(2)}, u32[]{:S(2)}) collective-permute-start(f32[200,512]{1,0:T(8,128)} %get-tuple-element.10), channel_id=1, source_target_pairs={{0,63},{1,0},{2,1},{3,2},{4,3},{5,4},{6,5},{7,6},{8,7},{9,8},{10,9... | collective-permute-start | bytes 1228808 | tf_op jit(solution)/shard_map/ppermute | solution.py:394
  6.3 0.0 collective-permute-start.1
  6.3 1.1 %collective-permute-start.2 = (f32[16,128]{1,0:T(8,128)}, f32[16,128]{1,0:T(8,128)S(1)}, u32[]{:S(2)}, u32[]{:S(2)}) collective-permute-start(f32[16,128]{1,0:T(8,128)} %get-tuple-element.12), channel_id=1, source_target_pairs={{0,64},{64,128},{128,192},{192,0},{1,65},{65,129},{129,193},{193,1... | collective-permute-start | bytes 24584 | tf_op jit(solution)/shard_map/ppermute | solution.py:397
  7.4 1.6 %collective-permute-start.3 = (f32[16,128]{1,0:T(8,128)}, f32[16,128]{1,0:T(8,128)S(1)}, u32[]{:S(2)}, u32[]{:S(2)}) collective-permute-start(f32[16,128]{1,0:T(8,128)} %get-tuple-element.13), channel_id=1, source_target_pairs={{0,192},{64,0},{128,64},{192,128},{1,193},{65,1},{129,65},{193,129... | collective-permute-start | bytes 24584 | tf_op jit(solution)/shard_map/ppermute | solution.py:396
  9.0 1.2 %collective-permute-done.2.left = f32[16,128]{1,0:T(8,128)S(1)} collective-permute-done((f32[16,128]{1,0:T(8,128)}, f32[16,128]{1,0:T(8,128)S(1)}, u32[]{:S(2)}, u32[]{:S(2)}) %collective-permute-start.2) | collective-permute-done | bytes 8224 | tf_op jit(solution)/shard_map/ppermute | solution.py:397
  10.2 0.0 copy-start.2
  10.2 0.6 copy-done.2
  10.8 0.0 collective-permute-done.3.right
  10.8 0.6 copy-done.3
  11.4 1.5 %collective-permute-start.5 = (f32[32,128]{1,0:T(8,128)S(1)}, f32[32,128]{1,0:T(8,128)S(1)}, u32[]{:S(2)}, u32[]{:S(2)}) collective-permute-start(f32[32,128]{1,0:T(8,128)S(1)} %constant_dynamic-update-slice_fusion), channel_id=1, source_target_pairs={{0,1},{1,2},{2,3},{3,4},{4,5},{5,6},{6,7},{7,8},{8,9},{9,10},{10,1... | collective-permute-start | bytes 49160 | tf_op jit(solution)/shard_map/ppermute | solution.py:400
  12.9 5.5 %collective-permute-start.4 = (f32[32,128]{1,0:T(8,128)S(1)}, f32[32,128]{1,0:T(8,128)S(1)}, u32[]{:S(2)}, u32[]{:S(2)}) collective-permute-start(f32[32,128]{1,0:T(8,128)S(1)} %constant_dynamic-update-slice_fusion), channel_id=1, source_target_pairs={{0,63},{1,0},{2,1},{3,2},{4,3},{5,4},{6,5},{7,6},{8,7},{9,8},{10,9... | collective-permute-start | bytes 49160 | tf_op jit(solution)/shard_map/ppermute | solution.py:399
  18.4 0.7 %collective-permute-done.5.above_corner = f32[32,128]{1,0:T(8,128)S(1)} collective-permute-done((f32[32,128]{1,0:T(8,128)S(1)}, f32[32,128]{1,0:T(8,128)S(1)}, u32[]{:S(2)}, u32[]{:S(2)}) %collective-permute-start.5) | collective-permute-done | bytes 16416 | tf_op jit(solution)/shard_map/ppermute | solution.py:400
  19.0 0.2 collective-permute-done.4.below_corner
  19.2 0.0 collective-permute-done.below
  19.2 0.0 collective-permute-done.1.above
  19.2 0.0 copy-start.1
  19.2 0.4 copy-done.4
  19.6 0.2 copy-done.5
  19.8 0.2 copy-done
  20.0 0.1 copy-done.1
  20.1 16.2 %terms.1 = (f32[8,4,8,512]{3,2,1,0:T(8,128)}, f32[256,128]{1,0:T(8,128)}) custom-call(f32[256,512]{1,0:T(8,128)} %get-tuple-element.9.first, f32[4,8,512]{2,1,0:T(8,128)} %onsite.3, f32[3,2,8,512]{3,2,1,0:T(8,128)} %intra.3, s32[4,2,8,512]{3,2,1,0:T(8,128)} %codes.3, f32[4,2,8,512]{3,2,1,0:T(8,128)} %inter.3, f32[200,512]{1,0:T(8,128)} %copy-done, ...), custom_call_target="tpu_custom_call" | custom-call | tf_op jit(solution)/shard_map/terms/pallas_call | solution.py:349
  36.3 28.4 %all_to_all.11 = f32[256,1,128]{2,1,0:T(1,128)} all-to-all(f32[256,1,128]{2,1,0:T(1,128)} %bitcast.5), channel_id=1, replica_groups=mesh['col'=4,'tile_0'=4,'tile_1'=8,'tile_2'=2] {'col','tile_0','tile_1',..., dimensions={0} | all-to-all | bytes 262144 | tf_op jit(solution)/shard_map/all_to_all | solution.py:405
  64.7 1.6 %finish.1 = f32[7,8]{1,0:T(8,128)} custom-call(f32[256,128]{1,0:T(8,128)} %bitcast.4), custom_call_target="tpu_custom_call" | custom-call | tf_op jit(solution)/shard_map/finish/pallas_call | solution.py:376
  (6 shorter events, 0.0 us)
Async XLA Ops:
  3.1 16.1 %collective-permute-start = (f32[200,512]{1,0:T(8,128)}, f32[200,512]{1,0:T(8,128)S(1)}, u32[]{:S(2)}, u32[]{:S(2)}) collective-permute-start(f32[200,512]{1,0:T(8,128)} %get-tuple-element.10), channel_id=1, source_target_pairs={{0,63},{1,0},{2,1},{3,2},{4,3},{5,4},{6,5},{7,6},{8,7},{9,8},{10,9... | collective-permute-start | bytes 1228808 | tf_op jit(solution)/shard_map/ppermute | solution.py:394
  6.3 12.9 %collective-permute-start.1 = (f32[200,512]{1,0:T(8,128)}, f32[200,512]{1,0:T(8,128)S(1)}, u32[]{:S(2)}, u32[]{:S(2)}) collective-permute-start(f32[200,512]{1,0:T(8,128)} %get-tuple-element.11), channel_id=1, source_target_pairs={{0,1},{1,2},{2,3},{3,4},{4,5},{5,6},{6,7},{7,8},{8,9},{9,10},{10,1... | collective-permute-start | bytes 1228808 | tf_op jit(solution)/shard_map/ppermute | solution.py:395
  6.3 3.9 %collective-permute-start.2 = (f32[16,128]{1,0:T(8,128)}, f32[16,128]{1,0:T(8,128)S(1)}, u32[]{:S(2)}, u32[]{:S(2)}) collective-permute-start(f32[16,128]{1,0:T(8,128)} %get-tuple-element.12), channel_id=1, source_target_pairs={{0,64},{64,128},{128,192},{192,0},{1,65},{65,129},{129,193},{193,1... | collective-permute-start | bytes 24584 | tf_op jit(solution)/shard_map/ppermute | solution.py:397
  7.4 3.4 %collective-permute-start.3 = (f32[16,128]{1,0:T(8,128)}, f32[16,128]{1,0:T(8,128)S(1)}, u32[]{:S(2)}, u32[]{:S(2)}) collective-permute-start(f32[16,128]{1,0:T(8,128)} %get-tuple-element.13), channel_id=1, source_target_pairs={{0,192},{64,0},{128,64},{192,128},{1,193},{65,1},{129,65},{193,129... | collective-permute-start | bytes 24584 | tf_op jit(solution)/shard_map/ppermute | solution.py:396
  10.2 0.6 copy-start.2
  10.8 0.6 copy-start.3
  11.4 7.6 %collective-permute-start.5 = (f32[32,128]{1,0:T(8,128)S(1)}, f32[32,128]{1,0:T(8,128)S(1)}, u32[]{:S(2)}, u32[]{:S(2)}) collective-permute-start(f32[32,128]{1,0:T(8,128)S(1)} %constant_dynamic-update-slice_fusion), channel_id=1, source_target_pairs={{0,1},{1,2},{2,3},{3,4},{4,5},{5,6},{6,7},{7,8},{8,9},{9,10},{10,1... | collective-permute-start | bytes 49160 | tf_op jit(solution)/shard_map/ppermute | solution.py:400
  12.9 6.3 %collective-permute-start.4 = (f32[32,128]{1,0:T(8,128)S(1)}, f32[32,128]{1,0:T(8,128)S(1)}, u32[]{:S(2)}, u32[]{:S(2)}) collective-permute-start(f32[32,128]{1,0:T(8,128)S(1)} %constant_dynamic-update-slice_fusion), channel_id=1, source_target_pairs={{0,63},{1,0},{2,1},{3,2},{4,3},{5,4},{6,5},{7,6},{8,7},{9,8},{10,9... | collective-permute-start | bytes 49160 | tf_op jit(solution)/shard_map/ppermute | solution.py:399
  19.0 0.6 copy-start.4
  19.2 0.6 copy-start.5
  19.2 0.8 %copy-start = (f32[200,512]{1,0:T(8,128)}, f32[200,512]{1,0:T(8,128)S(1)}, u32[]{:S(2)}) copy-start(f32[200,512]{1,0:T(8,128)S(1)} %collective-permute-done.below) | copy-start | bytes 1228804
  19.2 0.9 %copy-start.1 = (f32[200,512]{1,0:T(8,128)}, f32[200,512]{1,0:T(8,128)S(1)}, u32[]{:S(2)}) copy-start(f32[200,512]{1,0:T(8,128)S(1)} %collective-permute-done.1.above) | copy-start | bytes 1228804

commit v2 on v1

v2 whole, which is shorter than its diff:
```python
import functools

import jax
import jax.numpy as jnp
from jax import lax
from jax.experimental import pallas as pl
from jax.experimental.pallas import tpu as pltpu
from jax.sharding import Mesh
from jax.sharding import PartitionSpec as P

TILE = ("tile_0", "tile_1", "tile_2")
EVERY = ("col",) + TILE

V = 8
R = 8
C = 512
W = C + 128
RING = 16
RIM = 3
COEFS = 26
LANES = 128
BLOCKS = C // LANES
LAST = LANES - 1
STEP = RING + 1
VMEM = pl.BlockSpec(memory_space=pltpu.VMEM)
FIELD_ROWS = 4 * RIM * V
ROW_MSG = FIELD_ROWS + COEFS * 4

FWD = 0
SHIFTED = 36
INTRA = 60
INTRA_SHIFTED = 66
ONSITE = 68
PLANES = 72
STRIDE = PLANES + 1
TABLE = (C // LANES + 1) * RING * STRIDE
FIELD = (3, 4 * STEP * V, W)

SIDE_CODES = [code for code in range(18) if code % 3 != 1]


def offsets(code):
    return code % 9 // 3 - 1, code % 3 - 1


def shifted_plane(source, code):
    if code % 3 == 1:
        return FWD + source * 18 + code
    return SHIFTED + source * 12 + SIDE_CODES.index(code)


def lanes_of(shape):
    return lax.broadcasted_iota(jnp.int32, shape, len(shape) - 1)


def subs_of(shape):
    return lax.broadcasted_iota(jnp.int32, shape, len(shape) - 2)


def lane_roll(array, amount):
    amount = amount % array.shape[-1]
    if amount == 0:
        return array
    return pltpu.roll(array, amount, axis=array.ndim - 1)


def pack_kernel(vec, onsite, intra, codes, inter, field, coefs, up_msg, down_msg, left_msg, right_msg):
    for orbital in range(4):
        for block in range(C // LANES):
            cols = slice(block * LANES, (block + 1) * LANES)
            turned = jnp.swapaxes(vec[:, orbital, :, cols], 0, 1)
            for row in range(R):
                field[pl.ds((orbital * R + row) * V, V), cols] = turned[row]
                if row < RIM:
                    up_msg[pl.ds((orbital * RIM + row) * V, V), cols] = turned[row]
                if row >= R - RIM:
                    at = row - (R - RIM)
                    down_msg[pl.ds((orbital * RIM + at) * V, V), cols] = turned[row]

    def plane(index):
        if index < 4:
            return onsite[index]
        if index < 10:
            return intra[(index - 4) // 2, (index - 4) % 2]
        if index < 18:
            return codes[(index - 10) // 2, (index - 10) % 2].astype(jnp.float32)
        return inter[(index - 18) // 2, (index - 18) % 2]

    for index in range(COEFS):
        coefs[pl.ds(index * R, R), :] = plane(index)

    low = subs_of((R, C)) < 4
    for pair in range(COEFS // 2):
        even, odd = plane(2 * pair), plane(2 * pair + 1)
        odd_turned = pltpu.roll(odd, 4, axis=0)
        rows = pl.ds(FIELD_ROWS + pair * R, R)
        up_msg[rows, :] = jnp.where(low, even, odd_turned)
        down_msg[rows, :] = jnp.where(low, odd_turned, even)

    lane = lanes_of((R, LANES))
    left = jnp.zeros((R, LANES), jnp.float32)
    right = jnp.zeros((R, LANES), jnp.float32)
    for slot in range(32):
        rows = pl.ds(slot * V, V)
        inside = (lane >= 4 * slot) & (lane < 4 * slot + 4)
        left = jnp.where(inside, lane_roll(field[rows, 0:LANES], 4 * slot), left)
        right = jnp.where(inside, lane_roll(field[rows, C - LANES : C], 4 * slot + 4), right)
    left_msg[0:8, :] = left
    right_msg[0:8, :] = right
    left = jnp.zeros((R, LANES), jnp.float32)
    right = jnp.zeros((R, LANES), jnp.float32)
    for slot in range(COEFS):
        values = plane(slot)
        inside = (lane >= 4 * slot) & (lane < 4 * slot + 4)
        left = jnp.where(inside, lane_roll(values[:, 0:LANES], 4 * slot), left)
        right = jnp.where(inside, lane_roll(values[:, C - LANES : C], 4 * slot + 4), right)
    left_msg[8:16, :] = left
    right_msg[8:16, :] = right


def pack(vectors, onsite, intra, codes, inter):
    f32 = jnp.float32
    return pl.pallas_call(
        pack_kernel,
        out_shape=(
            jax.ShapeDtypeStruct((4 * R * V, C), f32),
            jax.ShapeDtypeStruct((COEFS * R, C), f32),
            jax.ShapeDtypeStruct((ROW_MSG, C), f32),
            jax.ShapeDtypeStruct((ROW_MSG, C), f32),
            jax.ShapeDtypeStruct((16, LANES), f32),
            jax.ShapeDtypeStruct((16, LANES), f32),
        ),
        out_specs=(VMEM,) * 6,
        compiler_params=pltpu.CompilerParams(vmem_limit_bytes=65190000),
        name="pack",
    )(vectors, onsite, intra, codes, inter)


def table_rows(plane, block, half):
    return pl.ds((block * RING + half * R) * STRIDE + plane, R, stride=STRIDE)


def planes_of(plane_at):
    kept = {}
    for index in range(4):
        kept[ONSITE + index] = 2.0 * plane_at(index)
    for index in range(6):
        kept[INTRA + index] = 2.0 * plane_at(4 + index)
    for source in range(2):
        marks = [plane_at(10 + 2 * k + source) for k in range(4)]
        hops = [2.0 * plane_at(18 + 2 * k + source) for k in range(4)]
        for code in range(18):
            terms = [jnp.where(m == float(code), h, 0.0) for m, h in zip(marks, hops)]
            kept[FWD + source * 18 + code] = (terms[0] + terms[1]) + (terms[2] + terms[3])
    return kept


def shifts():
    for source in range(2):
        for code in SIDE_CODES:
            yield FWD + source * 18 + code, shifted_plane(source, code), offsets(code)[1]
    for layer in range(2):
        yield INTRA + 4 + layer, INTRA_SHIFTED + layer, -1


def put_half(table, half, plane_at):
    kept = []
    for block in range(BLOCKS):
        kept.append(planes_of(lambda index: plane_at(index, block)))
        for plane, values in kept[-1].items():
            table[table_rows(plane, block, half), :] = values
    for plane, shifted, amount in shifts():
        row = lane_roll(jnp.concatenate([planes[plane] for planes in kept], axis=1), amount)
        for block in range(BLOCKS):
            at = table_rows(shifted, block, half)
            table[at, :] = row[:, block * LANES : (block + 1) * LANES]


def field_rows(orbital, row):
    start = (orbital * STEP + row) * V
    if not isinstance(start, int):
        start = pl.multiple_of(start, V)
    return pl.ds(start, V)


def put_middle(field, orbital, row, values):
    rows = field_rows(orbital, row)
    field[1, rows, 0:C] = values
    field[0, rows, 0:C] = lane_roll(values, 1)
    field[2, rows, 0:C] = lane_roll(values, -1)


def swap_in(amount, rim, turned, lane):
    rolled = lane_roll(rim, amount)
    outer = lane == (0 if amount == 1 else LAST)
    return jnp.where(outer, rolled, turned), jnp.where(outer, turned, rolled)


def own_kernel(first, coefs, zero, table):
    for orbital in range(4):
        for row in range(R):
            put_middle(zero, orbital, row, first[pl.ds((orbital * R + row) * V, V), :])

    def plane_at(index, block):
        return coefs[pl.ds(index * R, R), block * LANES : (block + 1) * LANES]

    put_half(table, 0, plane_at)


def own(field, coefs):
    f32 = jnp.float32
    return pl.pallas_call(
        own_kernel,
        out_shape=(
            jax.ShapeDtypeStruct(FIELD, f32),
            jax.ShapeDtypeStruct((TABLE, LANES), f32),
        ),
        in_specs=[VMEM] * 2,
        out_specs=(VMEM,) * 2,
        compiler_params=pltpu.CompilerParams(vmem_limit_bytes=4 << 20),
        cost_estimate=pl.CostEstimate(flops=4000000, bytes_accessed=4000000, transcendentals=0),
        name="own",
    )(field, coefs)


def near_kernel(zero_in, table_in, below, above, zero, table):
    for orbital in range(4):
        for at in range(RIM):
            rows = pl.ds((orbital * RIM + at) * V, V)
            put_middle(zero, orbital, R + at, below[rows, :])
            put_middle(zero, orbital, RING - RIM + at, above[rows, :])
    low = subs_of((R, LANES)) < 4

    def plane_at(index, block):
        cols = slice(block * LANES, (block + 1) * LANES)
        rows = pl.ds(FIELD_ROWS + index // 2 * R, R)
        if index % 2 == 0:
            return jnp.where(low, below[rows, cols], above[rows, cols])
        return pltpu.roll(jnp.where(low, above[rows, cols], below[rows, cols]), 4, axis=0)

    put_half(table, 1, plane_at)


def near(zero, table, below, above):
    f32 = jnp.float32
    return pl.pallas_call(
        near_kernel,
        out_shape=(
            jax.ShapeDtypeStruct(FIELD, f32),
            jax.ShapeDtypeStruct((TABLE, LANES), f32),
        ),
        in_specs=[VMEM] * 4,
        out_specs=(VMEM,) * 2,
        input_output_aliases={0: 0, 1: 1},
        compiler_params=pltpu.CompilerParams(vmem_limit_bytes=4 << 20),
        cost_estimate=pl.CostEstimate(flops=4000000, bytes_accessed=4000000, transcendentals=0),
        name="near",
    )(zero, table, below, above)


def put_rims(zero, table, left, right, below_corner, above_corner):
    low = subs_of((R, LANES)) < 4
    lane = lanes_of((R, LANES))
    left, right = left[...], right[...]
    below_corner, above_corner = below_corner[...], above_corner[...]

    def rim_of(sides, slot):
        return jnp.where(
            lane < 64, lane_roll(sides[1], -4 * slot), lane_roll(sides[0], 124 - 4 * slot)
        )

    def edges(rows, shift):
        return (
            (left[rows, :], right[rows, :]),
            (below_corner[rows, :], below_corner[shift, :]),
            (above_corner[rows, :], above_corner[shift, :]),
        )

    own_v, below_v, above_v = edges(slice(0, 8), slice(16, 24))
    ring_rows = list(range(R + RIM)) + list(range(RING - RIM, RING))
    for orbital in range(4):
        stores = []
        for row in ring_rows:
            sides = own_v if row < R else below_v if row < R + RIM else above_v
            rim = rim_of(sides, orbital * 8 + row % 8)
            rows = field_rows(orbital, row)
            first_edge, first_rim = swap_in(1, rim, zero[0, rows, 0:LANES], lane)
            last_edge, last_rim = swap_in(-1, rim, zero[2, rows, C - LANES : C], lane)
            stores.append((rows, rim, first_edge, first_rim, last_edge, last_rim))
        for rows, rim, first_edge, first_rim, last_edge, last_rim in stores:
            zero[1, rows, C:W] = rim
            zero[0, rows, 0:LANES] = first_edge
            zero[0, rows, C:W] = first_rim
            zero[2, rows, C - LANES : C] = last_edge
            zero[2, rows, C:W] = last_rim

    own_c, below_c, above_c = edges(slice(8, 16), slice(24, 32))
    near_c = [jnp.where(low, b, a) for b, a in zip(below_c, above_c)]
    stores = []
    for half in range(2):
        rims = [rim_of((own_c, near_c)[half], index) for index in range(COEFS)]
        kept = planes_of(rims.__getitem__)
        for plane, values in kept.items():
            stores.append((table_rows(plane, BLOCKS, half), values))
        for plane, shifted, amount in shifts():
            at = table_rows(shifted, 0 if amount == 1 else BLOCKS - 1, half)
            edge, outer = swap_in(amount, kept[plane], table[at, :], lane)
            stores.append((at, edge))
            stores.append((table_rows(shifted, BLOCKS, half), outer))
    for at, values in stores:
        table[at, :] = values


def stencil_pair(field, table, row, block):
    cols = slice(block * LANES, (block + 1) * LANES)
    at = {step: (row + step) & (RING - 1) for step in range(-1, 3)}
    start = {step: (block * RING + at[step]) * STRIDE for step in at}
    sums = [[None] * 4 for _ in range(2)]

    def add(cell, orbital, plane, step, value):
        coef = table[pl.ds(start[step] + plane, V, stride=0), :]
        term = coef * value
        old = sums[cell][orbital]
        sums[cell][orbital] = term if old is None else old + term

    for step in range(-1, 3):
        for col_off in (-1, 0, 1):
            value = [field[1 + col_off, field_rows(o, at[step]), cols] for o in range(4)]
            for cell in range(2):
                row_off = step - cell
                if abs(row_off) > 1:
                    continue
                code = (row_off + 1) * 3 + col_off + 1
                back = (1 - row_off) * 3 + 1 - col_off
                for source in range(2):
                    for target in range(2):
                        plane = FWD + source * 18 + 9 * target + code
                        add(cell, source, plane, cell, value[2 + target])
                        plane = shifted_plane(source, 9 * target + back)
                        add(cell, 2 + target, plane, step, value[source])
                for layer in range(2):
                    a, b = 2 * layer, 2 * layer + 1
                    if (row_off, col_off) == (0, 0):
                        add(cell, a, ONSITE + a, cell, value[a])
                        add(cell, b, ONSITE + b, cell, value[b])
                        add(cell, a, INTRA + layer, cell, value[b])
                        add(cell, b, INTRA + layer, cell, value[a])
                    elif (row_off, col_off) == (-1, 0):
                        add(cell, a, INTRA + 2 + layer, cell, value[b])
                    elif (row_off, col_off) == (1, 0):
                        add(cell, b, INTRA + 2 + layer, step, value[a])
                    elif (row_off, col_off) == (0, -1):
                        add(cell, a, INTRA + 4 + layer, cell, value[b])
                    elif (row_off, col_off) == (0, 1):
                        add(cell, b, INTRA_SHIFTED + layer, cell, value[a])
    return sums


def term_rows(source, target, table, row, value_of):
    lane = lanes_of((V, LANES))
    count = BLOCKS + 1
    keys = [(cell, orbital) for cell in range(2) for orbital in range(4)]
    rows = {key: field_rows(key[1], (row + key[0]) & (RING - 1)) for key in keys}
    up, down = {}, {}

    def columns(block):
        return slice(block * LANES, (block + 1) * LANES)

    def put_up(block):
        for key in keys:
            inner = up[key, block]
            target[0, rows[key], columns(block)] = jnp.where(
                lane == 0, up[key, (block - 1) % count], inner
            )

    def put_down(block):
        for key in keys:
            inner = down[key, block]
            target[2, rows[key], columns(block)] = jnp.where(
                lane == LAST, down[key, (block + 1) % count], inner
            )

    order = [BLOCKS] + list(range(BLOCKS))
    for at, block in enumerate(order):
        result = stencil_pair(source, table, row, block)
        for key in keys:
            value = value_of(result[key[0]][key[1]], rows[key], columns(block))
            target[1, rows[key], columns(block)] = value
            up[key, block] = lane_roll(value, 1)
            down[key, block] = lane_roll(value, -1)
        if at > 0:
            put_up(block)
            put_down(order[at - 1])
    put_up(order[0])
    put_down(order[-1])


def terms_kernel(
    zero_in, table_in, left, right, below_corner, above_corner,
    out, partial, zero, table, one, two, last
):
    lane = lanes_of((V, LANES))
    put_rims(zero, table, left, right, below_corner, above_corner)

    def first_rows(step, carry):
        row = (2 * step - 2) & (RING - 1)
        term_rows(zero, one, table, row, lambda sum_, rows, cols: 0.5 * sum_)
        return carry

    lax.fori_loop(0, R // 2 + 2, first_rows, 0)

    def second_rows(step, carry):
        row = (2 * step - 1) & (RING - 1)
        term_rows(one, two, table, row, lambda sum_, rows, cols: sum_ - zero[1, rows, cols])
        return carry

    lax.fori_loop(0, R // 2 + 1, second_rows, 0)

    def third_rows(step, sums):
        row = 2 * step
        sums = list(sums)
        for block in range(BLOCKS):
            cols = slice(block * LANES, (block + 1) * LANES)
            result = stencil_pair(two, table, row, block)
            for cell in range(2):
                for orbital in range(4):
                    rows = field_rows(orbital, row + cell)
                    t0 = zero[1, rows, cols]
                    t1 = one[1, rows, cols]
                    t2 = two[1, rows, cols]
                    t3 = result[cell][orbital] - t1
                    at = pl.multiple_of((orbital * R + row + cell) * V, V)
                    last[pl.ds(at, V), cols] = t3
                    for at, (x, y) in enumerate(
                        ((t0, t0), (t1, t0), (t1, t1), (t2, t1), (t2, t2), (t3, t2), (t3, t3))
                    ):
                        sums[at] = sums[at] + x * y
        return tuple(sums)

    empty = jnp.zeros((V, LANES), jnp.float32)
    sums = lax.fori_loop(0, R // 2, third_rows, (empty,) * 7)

    for orbital in range(4):
        for block in range(BLOCKS):
            cols = slice(block * LANES, (block + 1) * LANES)
            rows = pl.ds(orbital * R * V, R * V)
            turned = jnp.swapaxes(last[rows, cols].reshape(R, V, LANES), 0, 1)
            out[:, orbital, :, cols] = turned

    spread = empty
    sub = subs_of((V, LANES))
    for at in range(7):
        total = jnp.sum(sums[at], axis=1, keepdims=True)
        spread = jnp.where(lane == 8 * at + sub, total, spread)
    line = jnp.sum(spread, axis=0, keepdims=True)
    partial[...] = jnp.broadcast_to(line, partial.shape)


def apply_terms(devices, *args):
    f32 = jnp.float32
    results = pl.pallas_call(
        terms_kernel,
        out_shape=(
            jax.ShapeDtypeStruct((V, 4, R, C), f32),
            jax.ShapeDtypeStruct((devices, LANES), f32),
            jax.ShapeDtypeStruct(FIELD, f32),
            jax.ShapeDtypeStruct((TABLE, LANES), f32),
        ),
        in_specs=[VMEM] * 6,
        out_specs=(VMEM,) * 4,
        input_output_aliases={0: 2, 1: 3},
        scratch_shapes=[
            pltpu.VMEM(FIELD, f32),
            pltpu.VMEM(FIELD, f32),
            pltpu.VMEM((4 * R * V, C), f32),
        ],
        compiler_params=pltpu.CompilerParams(vmem_limit_bytes=16 << 20),
        name="terms",
    )(*args)
    return results[0], results[1]


def finish_kernel(orbitals, parts, out):
    line = jnp.sum(parts[...], axis=0, keepdims=True) / orbitals
    rows = [lane_roll(line, -8 * at)[:, 0:V] for at in range(7)]
    out[0:1, :] = rows[0]
    out[1:2, :] = rows[1]
    for at in range(2, 7):
        out[at : at + 1, :] = 2.0 * rows[at] - rows[at % 2]


def finish(parts, orbitals):
    return pl.pallas_call(
        functools.partial(finish_kernel, orbitals),
        out_shape=jax.ShapeDtypeStruct((7, V), jnp.float32),
        in_specs=[VMEM],
        out_specs=VMEM,
        compiler_params=pltpu.CompilerParams(vmem_limit_bytes=1 << 20),
        name="finish",
    )(parts)


def on_device(vectors, onsite, intra_hop, inter_index, inter_hop):
    cols = lax.axis_size("col")
    tiles = lax.axis_size(TILE)
    devices = cols * tiles

    def ring(count, step):
        return [(i, (i + step) % count) for i in range(count)]

    field, coefs, up_msg, down_msg, left_msg, right_msg = pack(
        vectors, onsite, intra_hop, inter_index, inter_hop
    )
    below = lax.ppermute(up_msg, TILE, ring(tiles, -1))
    above = lax.ppermute(down_msg, TILE, ring(tiles, 1))
    right = lax.ppermute(left_msg, "col", ring(cols, -1))
    left = lax.ppermute(right_msg, "col", ring(cols, 1))
    zero, table = own(field, coefs)
    corner = jnp.concatenate([left, right], axis=0)
    below_corner = lax.ppermute(corner, TILE, ring(tiles, -1))
    above_corner = lax.ppermute(corner, TILE, ring(tiles, 1))
    zero, table = near(zero, table, below, above)
    last_term, partial = apply_terms(
        devices, zero, table, left, right, below_corner, above_corner
    )
    parts = lax.all_to_all(partial, EVERY, 0, 0)
    return last_term, finish(parts, 4.0 * R * C * devices)


def solution(mesh):
    torus = Mesh(
        mesh.devices.reshape(mesh.shape["col"], 4, 8, 2), ("col", "tile_0", "tile_1", "tile_2")
    )
    placed = (
        P(None, None, TILE, "col"),
        P(None, TILE, "col"),
        P(None, None, TILE, "col"),
        P(None, None, TILE, "col"),
        P(None, None, TILE, "col"),
    )
    return jax.shard_map(
        on_device,
        mesh=torus,
        in_specs=placed,
        out_specs=(P(None, None, TILE, "col"), P()),
        check_vma=False,
    )
```

time: 66.5 us -> 57.7 us (0.87)
  Pallas kernels: 20.3 us -> 14.7 us
  blocking collectives: 28.4 us -> 24.4 us
    pallas_call x1 -> x3, Pallas kernels: 16.2 us -> 11.4 us  [the longest x1 10.4 us: apply_terms(): pl.pallas_call(terms_kernel, out_shape=(jax.ShapeDtypeStruct((V, 4, R, C)...]
    all_to_all x1, blocking collectives: 28.4 us -> 24.4 us  [on_device(): parts = lax.all_to_all(partial, EVERY, 0, 0)]
    ppermute x1, starting transfers between devices: 5.46 us -> 7.29 us  [on_device(): below_corner = lax.ppermute(corner, TILE, ring(tiles, -1))]
    ppermute x1, starting transfers between devices: 1.47 us -> 0.01 us  [on_device(): above_corner = lax.ppermute(corner, TILE, ring(tiles, 1))]
    pallas_call x1, Pallas kernels: 1.61 us -> 0.71 us  [finish(): pl.pallas_call(functools.partial(finish_kernel, orbitals), out_shape=jax....]
    unnamed x13 -> x5, local copies, waits for them, and re-layouts: 2.06 us -> 2.05 us
  transfers between devices with their start and end apart: 6 -> 6, of which waited for: 3 -> 2; matrix products, arithmetic and copies ran while one was open for 0% -> 0% of each run, Pallas kernels for 0% -> 2%
where the time goes in v2:
time: 57.7 us; the launch traced here: 57.5 us
  blocking collectives  24.4 us (42%)
  Pallas kernels  14.7 us (25%)
  starting transfers between devices  13.2 us (23%)
  waiting for transfers between devices  2.47 us (4%)
  local copies, waits for them, and re-layouts  2.05 us (4%)
  between operations  0.68 us (1%)
    all_to_all x1, blocking collectives, on_device(): parts = lax.all_to_all(partial, EVERY, 0, 0)  24.4 us
    pallas_call x1, Pallas kernels, apply_terms(): pl.pallas_call(terms_kernel, out_shape=(jax.ShapeDtypeStruct((V, 4, R, C)...  10.4 us
    ppermute x1, starting transfers between devices, on_device(): below_corner = lax.ppermute(corner, TILE, ring(tiles, -1))  7.29 us
    ppermute x1, starting transfers between devices, on_device(): below = lax.ppermute(up_msg, TILE, ring(tiles, -1))  3.2 us
    pallas_call x1, Pallas kernels, pack(): pl.pallas_call(pack_kernel, out_shape=(jax.ShapeDtypeStruct((4 * R * V, C...  2.57 us
    unnamed x5, local copies, waits for them, and re-layouts  2.05 us
    ppermute x1, starting transfers between devices, on_device(): right = lax.ppermute(left_msg, 'col', ring(cols, -1))  1.52 us
    ppermute x1, waiting for transfers between devices, on_device(): left = lax.ppermute(right_msg, 'col', ring(cols, 1))  1.25 us
  transfers between devices with their start and end apart: 6, of which 2 were waited for; matrix products, arithmetic and copies ran while one was open for 0% of the time, Pallas kernels for 2%

profile of v2, /device:TPU:1, one launch (start us, length us, event | category | flops | bytes accessed | tf_op | source)
XLA Modules:
  0.0 57.5 jit_solution(5704404085841272610)
XLA Ops:
  0.6 2.6 %pack.1 = (f32[256,512]{1,0:T(8,128)}, f32[208,512]{1,0:T(8,128)}, f32[200,512]{1,0:T(8,128)}, f32[200,512]{1,0:T(8,128)}, f32[16,128]{1,0:T(8,128)}, /*index=5*/f32[16,128]{1,0:T(8,128)}) custom-call(f32[8,4,8,512]{3,2,1,0:T(8,128)} %vec.1, f32[4,8,512]{2,1,0:T(8,128)} %onsite.1, f32[3,2,8,512]{3,2,1,0:T(8,128)} %intra.1, s32[4,2,8,512]{3,2,1,0:T(8,128)} %codes.1, ...), custom_call_target="tpu_custom_call" | custom-call | tf_op jit(solution)/shard_map/pack/pallas_call | solution.py:123
  3.2 3.2 %collective-permute-start = (f32[200,512]{1,0:T(8,128)}, f32[200,512]{1,0:T(8,128)S(1)}, u32[]{:S(2)}, u32[]{:S(2)}) collective-permute-start(f32[200,512]{1,0:T(8,128)} %get-tuple-element.18), channel_id=1, source_target_pairs={{0,63},{1,0},{2,1},{3,2},{4,3},{5,4},{6,5},{7,6},{8,7},{9,8},{10,9... | collective-permute-start | bytes 1228808 | tf_op jit(solution)/shard_map/ppermute | solution.py:514
  6.4 0.0 collective-permute-start.1
  6.4 1.2 %collective-permute-start.2 = (f32[16,128]{1,0:T(8,128)}, f32[16,128]{1,0:T(8,128)S(1)}, u32[]{:S(2)}, u32[]{:S(2)}) collective-permute-start(f32[16,128]{1,0:T(8,128)} %get-tuple-element.22), channel_id=1, source_target_pairs={{0,64},{64,128},{128,192},{192,0},{1,65},{65,129},{129,193},{193,1... | collective-permute-start | bytes 24584 | tf_op jit(solution)/shard_map/ppermute | solution.py:517
  7.6 1.5 %collective-permute-start.3 = (f32[16,128]{1,0:T(8,128)}, f32[16,128]{1,0:T(8,128)S(1)}, u32[]{:S(2)}, u32[]{:S(2)}) collective-permute-start(f32[16,128]{1,0:T(8,128)} %get-tuple-element.23), channel_id=1, source_target_pairs={{0,192},{64,0},{128,64},{192,128},{1,193},{65,1},{129,65},{193,129... | collective-permute-start | bytes 24584 | tf_op jit(solution)/shard_map/ppermute | solution.py:516
  9.1 1.2 %collective-permute-done.2.left = f32[16,128]{1,0:T(8,128)S(1)} collective-permute-done((f32[16,128]{1,0:T(8,128)}, f32[16,128]{1,0:T(8,128)S(1)}, u32[]{:S(2)}, u32[]{:S(2)}) %collective-permute-start.2) | collective-permute-done | bytes 8224 | tf_op jit(solution)/shard_map/ppermute | solution.py:517
  10.3 0.0 collective-permute-done.3.right
  10.3 7.3 %collective-permute-start.4 = (f32[32,128]{1,0:T(8,128)S(1)}, f32[32,128]{1,0:T(8,128)S(1)}, u32[]{:S(2)}, u32[]{:S(2)}) collective-permute-start(f32[32,128]{1,0:T(8,128)S(1)} %constant_dynamic-update-slice_fusion), channel_id=1, source_target_pairs={{0,63},{1,0},{2,1},{3,2},{4,3},{5,4},{6,5},{7,6},{8,7},{9,8},{10,9... | collective-permute-start | bytes 49160 | tf_op jit(solution)/shard_map/ppermute | solution.py:520
  17.6 0.0 collective-permute-start.5
  17.6 0.0 copy-start
  17.6 1.0 %copy-done = f32[256,512]{1,0:T(8,128)S(1)} copy-done((f32[256,512]{1,0:T(8,128)S(1)}, f32[256,512]{1,0:T(8,128)}, u32[]{:S(2)}) %copy-start) | copy-done | bytes 524312
  18.7 0.0 copy-start.1
  18.7 1.0 %copy-done.1 = f32[208,512]{1,0:T(8,128)S(1)} copy-done((f32[208,512]{1,0:T(8,128)S(1)}, f32[208,512]{1,0:T(8,128)}, u32[]{:S(2)}) %copy-start.1) | copy-done | bytes 426008
  19.7 0.5 own.1
  20.2 0.0 collective-permute-done.below
  20.2 0.0 collective-permute-done.1.above
  20.3 0.5 near.1
  20.8 0.0 collective-permute-done.4.below_corner
  20.8 1.2 %collective-permute-done.5.above_corner = f32[32,128]{1,0:T(8,128)S(1)} collective-permute-done((f32[32,128]{1,0:T(8,128)S(1)}, f32[32,128]{1,0:T(8,128)S(1)}, u32[]{:S(2)}, u32[]{:S(2)}) %collective-permute-start.5) | collective-permute-done | bytes 16416 | tf_op jit(solution)/shard_map/ppermute | solution.py:521
  22.0 10.4 %terms.1 = (f32[8,4,8,512]{3,2,1,0:T(8,128)}, f32[256,128]{1,0:T(8,128)S(1)}, f32[3,544,640]{2,1,0:T(8,128)S(1)}, f32[5840,128]{1,0:T(8,128)S(1)}) custom-call(f32[3,544,640]{2,1,0:T(8,128)S(1)} %get-tuple-element.20.zero_in, f32[5840,128]{1,0:T(8,128)S(1)} %get-tuple-element.21.table_in, ...), custom_call_target="tpu_custom_call", output_to_operand_aliasing={{2}: (0, {}), {3}: (1, {})} | custom-call | tf_op jit(solution)/shard_map/terms/pallas_call | solution.py:461
  32.3 24.4 %all_to_all.11 = f32[256,1,128]{2,1,0:T(1,128)S(1)} all-to-all(f32[256,1,128]{2,1,0:T(1,128)S(1)} %bitcast.5), channel_id=1, replica_groups=mesh['col'=4,'tile_0'=4,'tile_1'=8,'tile_2'=2] {'col','tile_0','tile_1',..., dimensions={0} | all-to-all | bytes 262144 | tf_op jit(solution)/shard_map/all_to_all | solution.py:526
  56.8 0.7 %finish.1 = f32[7,8]{1,0:T(8,128)} custom-call(f32[256,128]{1,0:T(8,128)S(1)} %bitcast.4), custom_call_target="tpu_custom_call" | custom-call | tf_op jit(solution)/shard_map/finish/pallas_call | solution.py:493
  (2 shorter events, 0.0 us)
Async XLA Ops:
  3.2 17.0 %collective-permute-start = (f32[200,512]{1,0:T(8,128)}, f32[200,512]{1,0:T(8,128)S(1)}, u32[]{:S(2)}, u32[]{:S(2)}) collective-permute-start(f32[200,512]{1,0:T(8,128)} %get-tuple-element.18), channel_id=1, source_target_pairs={{0,63},{1,0},{2,1},{3,2},{4,3},{5,4},{6,5},{7,6},{8,7},{9,8},{10,9... | collective-permute-start | bytes 1228808 | tf_op jit(solution)/shard_map/ppermute | solution.py:514
  6.4 13.9 %collective-permute-start.1 = (f32[200,512]{1,0:T(8,128)}, f32[200,512]{1,0:T(8,128)S(1)}, u32[]{:S(2)}, u32[]{:S(2)}) collective-permute-start(f32[200,512]{1,0:T(8,128)} %get-tuple-element.19), channel_id=1, source_target_pairs={{0,1},{1,2},{2,3},{3,4},{4,5},{5,6},{6,7},{7,8},{8,9},{9,10},{10,1... | collective-permute-start | bytes 1228808 | tf_op jit(solution)/shard_map/ppermute | solution.py:515
  6.4 3.9 %collective-permute-start.2 = (f32[16,128]{1,0:T(8,128)}, f32[16,128]{1,0:T(8,128)S(1)}, u32[]{:S(2)}, u32[]{:S(2)}) collective-permute-start(f32[16,128]{1,0:T(8,128)} %get-tuple-element.22), channel_id=1, source_target_pairs={{0,64},{64,128},{128,192},{192,0},{1,65},{65,129},{129,193},{193,1... | collective-permute-start | bytes 24584 | tf_op jit(solution)/shard_map/ppermute | solution.py:517
  7.6 2.8 %collective-permute-start.3 = (f32[16,128]{1,0:T(8,128)}, f32[16,128]{1,0:T(8,128)S(1)}, u32[]{:S(2)}, u32[]{:S(2)}) collective-permute-start(f32[16,128]{1,0:T(8,128)} %get-tuple-element.23), channel_id=1, source_target_pairs={{0,192},{64,0},{128,64},{192,128},{1,193},{65,1},{129,65},{193,129... | collective-permute-start | bytes 24584 | tf_op jit(solution)/shard_map/ppermute | solution.py:516
  10.3 10.4 %collective-permute-start.4 = (f32[32,128]{1,0:T(8,128)S(1)}, f32[32,128]{1,0:T(8,128)S(1)}, u32[]{:S(2)}, u32[]{:S(2)}) collective-permute-start(f32[32,128]{1,0:T(8,128)S(1)} %constant_dynamic-update-slice_fusion), channel_id=1, source_target_pairs={{0,63},{1,0},{2,1},{3,2},{4,3},{5,4},{6,5},{7,6},{8,7},{9,8},{10,9... | collective-permute-start | bytes 49160 | tf_op jit(solution)/shard_map/ppermute | solution.py:520
  17.6 4.4 %collective-permute-start.5 = (f32[32,128]{1,0:T(8,128)S(1)}, f32[32,128]{1,0:T(8,128)S(1)}, u32[]{:S(2)}, u32[]{:S(2)}) collective-permute-start(f32[32,128]{1,0:T(8,128)S(1)} %constant_dynamic-update-slice_fusion), channel_id=1, source_target_pairs={{0,1},{1,2},{2,3},{3,4},{4,5},{5,6},{6,7},{7,8},{8,9},{9,10},{10,1... | collective-permute-start | bytes 49160 | tf_op jit(solution)/shard_map/ppermute | solution.py:521
  17.6 1.0 %copy-start = (f32[256,512]{1,0:T(8,128)S(1)}, f32[256,512]{1,0:T(8,128)}, u32[]{:S(2)}) copy-start(f32[256,512]{1,0:T(8,128)} %get-tuple-element.14.first) | copy-start | bytes 1572868
  18.7 1.0 %copy-start.1 = (f32[208,512]{1,0:T(8,128)S(1)}, f32[208,512]{1,0:T(8,128)}, u32[]{:S(2)}) copy-start(f32[208,512]{1,0:T(8,128)} %get-tuple-element.15.coefs) | copy-start | bytes 1277956

commit v3 on v2

--- a/solution.py
+++ b/solution.py
@@ -7,6 +7,7 @@
 from jax.experimental.pallas import tpu as pltpu
 from jax.sharding import Mesh
 from jax.sharding import PartitionSpec as P
+
 
 TILE = ("tile_0", "tile_1", "tile_2")
 EVERY = ("col",) + TILE
@@ -64,7 +65,7 @@
     return pltpu.roll(array, amount, axis=array.ndim - 1)
 
 
-def pack_kernel(vec, onsite, intra, codes, inter, field, coefs, up_msg, down_msg, left_msg, right_msg):
+def pack_kernel(vec, onsite, intra, codes, inter, field, coefs, up_msg, down_msg, edge_msg):
     for orbital in range(4):
         for block in range(C // LANES):
             cols = slice(block * LANES, (block + 1) * LANES)
@@ -98,24 +99,21 @@
         down_msg[rows, :] = jnp.where(low, odd_turned, even)
 
     lane = lanes_of((R, LANES))
-    left = jnp.zeros((R, LANES), jnp.float32)
-    right = jnp.zeros((R, LANES), jnp.float32)
-    for slot in range(32):
-        rows = pl.ds(slot * V, V)
-        inside = (lane >= 4 * slot) & (lane < 4 * slot + 4)
-        left = jnp.where(inside, lane_roll(field[rows, 0:LANES], 4 * slot), left)
-        right = jnp.where(inside, lane_roll(field[rows, C - LANES : C], 4 * slot + 4), right)
-    left_msg[0:8, :] = left
-    right_msg[0:8, :] = right
-    left = jnp.zeros((R, LANES), jnp.float32)
-    right = jnp.zeros((R, LANES), jnp.float32)
-    for slot in range(COEFS):
-        values = plane(slot)
-        inside = (lane >= 4 * slot) & (lane < 4 * slot + 4)
-        left = jnp.where(inside, lane_roll(values[:, 0:LANES], 4 * slot), left)
-        right = jnp.where(inside, lane_roll(values[:, C - LANES : C], 4 * slot + 4), right)
-    left_msg[8:16, :] = left
-    right_msg[8:16, :] = right
+
+    def pack_edges(count, block_of):
+        packed = [jnp.zeros((R, LANES), jnp.float32) for _ in range(2)]
+        for slot in range(count):
+            ends = jnp.where(lane < 64, block_of(slot, 0), block_of(slot, C - LANES))
+            inside = ((lane + 4) & LAST) >> 3 == slot % 16
+            packed[slot // 16] = jnp.where(
+                inside, lane_roll(ends, 8 * slot), packed[slot // 16]
+            )
+        return packed
+
+    packed = pack_edges(32, lambda slot, at: field[pl.ds(slot * V, V), at : at + LANES])
+    packed += pack_edges(COEFS, lambda slot, at: coefs[pl.ds(slot * R, R), at : at + LANES])
+    for at, values in enumerate(packed):
+        edge_msg[at * 8 : at * 8 + 8, :] = values
 
 
 def pack(vectors, onsite, intra, codes, inter):
@@ -127,13 +125,17 @@
             jax.ShapeDtypeStruct((COEFS * R, C), f32),
             jax.ShapeDtypeStruct((ROW_MSG, C), f32),
             jax.ShapeDtypeStruct((ROW_MSG, C), f32),
-            jax.ShapeDtypeStruct((16, LANES), f32),
-            jax.ShapeDtypeStruct((16, LANES), f32),
+            jax.ShapeDtypeStruct((32, LANES), f32),
         ),
-        out_specs=(VMEM,) * 6,
-        compiler_params=pltpu.CompilerParams(vmem_limit_bytes=65190000),
+        out_specs=(VMEM,) * 5,
+        compiler_params=pltpu.CompilerParams(vmem_limit_bytes=16 << 20),
         name="pack",
-    )(vectors, onsite, intra, codes, inter)
+    )(
+        *(
+            pltpu.with_memory_space_constraint(array, pltpu.HBM)
+            for array in (vectors, onsite, intra, codes, inter)
+        )
+    )
 
 
 def table_rows(plane, block, half):
@@ -190,8 +192,7 @@
     field[2, rows, 0:C] = lane_roll(values, -1)
 
 
-def swap_in(amount, rim, turned, lane):
-    rolled = lane_roll(rim, amount)
+def swap_in(amount, rolled, turned, lane):
     outer = lane == (0 if amount == 1 else LAST)
     return jnp.where(outer, rolled, turned), jnp.where(outer, turned, rolled)
 
@@ -258,57 +259,52 @@
     )(zero, table, below, above)
 
 
-def put_rims(zero, table, left, right, below_corner, above_corner):
-    low = subs_of((R, LANES)) < 4
-    lane = lanes_of((R, LANES))
-    left, right = left[...], right[...]
-    below_corner, above_corner = below_corner[...], above_corner[...]
-
-    def rim_of(sides, slot):
-        return jnp.where(
-            lane < 64, lane_roll(sides[1], -4 * slot), lane_roll(sides[0], 124 - 4 * slot)
-        )
-
-    def edges(rows, shift):
-        return (
-            (left[rows, :], right[rows, :]),
-            (below_corner[rows, :], below_corner[shift, :]),
-            (above_corner[rows, :], above_corner[shift, :]),
-        )
-
-    own_v, below_v, above_v = edges(slice(0, 8), slice(16, 24))
-    ring_rows = list(range(R + RIM)) + list(range(RING - RIM, RING))
+def put_field_rims(zero, edges, ring_rows):
+    lane = lanes_of((V, LANES))
     for orbital in range(4):
         stores = []
         for row in ring_rows:
-            sides = own_v if row < R else below_v if row < R + RIM else above_v
-            rim = rim_of(sides, orbital * 8 + row % 8)
+            slot = orbital * 8 + row % 8
+            rims = [lane_roll(edges[slot // 16], amount - 8 * slot) for amount in (1, 0, -1)]
             rows = field_rows(orbital, row)
-            first_edge, first_rim = swap_in(1, rim, zero[0, rows, 0:LANES], lane)
-            last_edge, last_rim = swap_in(-1, rim, zero[2, rows, C - LANES : C], lane)
-            stores.append((rows, rim, first_edge, first_rim, last_edge, last_rim))
-        for rows, rim, first_edge, first_rim, last_edge, last_rim in stores:
+            first = swap_in(1, rims[0], zero[0, rows, 0:LANES], lane)
+            last = swap_in(-1, rims[2], zero[2, rows, C - LANES : C], lane)
+            stores.append((rows, rims[1], first, last))
+        for rows, rim, first, last in stores:
             zero[1, rows, C:W] = rim
-            zero[0, rows, 0:LANES] = first_edge
-            zero[0, rows, C:W] = first_rim
-            zero[2, rows, C - LANES : C] = last_edge
-            zero[2, rows, C:W] = last_rim
-
-    own_c, below_c, above_c = edges(slice(8, 16), slice(24, 32))
-    near_c = [jnp.where(low, b, a) for b, a in zip(below_c, above_c)]
-    stores = []
-    for half in range(2):
-        rims = [rim_of((own_c, near_c)[half], index) for index in range(COEFS)]
-        kept = planes_of(rims.__getitem__)
-        for plane, values in kept.items():
-            stores.append((table_rows(plane, BLOCKS, half), values))
-        for plane, shifted, amount in shifts():
-            at = table_rows(shifted, 0 if amount == 1 else BLOCKS - 1, half)
-            edge, outer = swap_in(amount, kept[plane], table[at, :], lane)
-            stores.append((at, edge))
-            stores.append((table_rows(shifted, BLOCKS, half), outer))
-    for at, values in stores:
-        table[at, :] = values
+            zero[0, rows, 0:LANES], zero[0, rows, C:W] = first
+            zero[2, rows, C - LANES : C], zero[2, rows, C:W] = last
+
+
+def put_table_rims(table, edges, half):
+    lane = lanes_of((R, LANES))
+
+    def rolled_by(amount):
+        return lambda index: lane_roll(edges[index // 16], amount - 8 * index)
+
+    for plane, values in planes_of(rolled_by(0)).items():
+        table[table_rows(plane, BLOCKS, half), :] = values
+    for amount in (1, -1):
+        rolled = planes_of(rolled_by(amount))
+        for plane, shifted, by in shifts():
+            if by == amount:
+                at = table_rows(shifted, 0 if amount == 1 else BLOCKS - 1, half)
+                edge, outer = swap_in(amount, rolled[plane], table[at, :], lane)
+                table[at, :] = edge
+                table[table_rows(shifted, BLOCKS, half), :] = outer
+
+
+def put_rims(zero, table, own_edge, below_edge, above_edge):
+    low = subs_of((R, LANES)) < 4
+    own, below, above = [
+        [ref[8 * at : 8 * at + 8, :] for at in range(4)]
+        for ref in (own_edge, below_edge, above_edge)
+    ]
+    put_field_rims(zero, own[:2], range(R))
+    put_field_rims(zero, below[:2], range(R, R + RIM))
+    put_field_rims(zero, above[:2], range(RING - RIM, RING))
+    put_table_rims(table, own[2:], 0)
+    put_table_rims(table, [jnp.where(low, b, a) for b, a in zip(below[2:], above[2:])], 1)
 
 
 def stencil_pair(field, table, row, block):
@@ -396,11 +392,11 @@
 
 
 def terms_kernel(
-    zero_in, table_in, left, right, below_corner, above_corner,
+    zero_in, table_in, own_edge, below_edge, above_edge,
     out, partial, zero, table, one, two, last
 ):
     lane = lanes_of((V, LANES))
-    put_rims(zero, table, left, right, below_corner, above_corner)
+    put_rims(zero, table, own_edge, below_edge, above_edge)
 
     def first_rows(step, carry):
         row = (2 * step - 2) & (RING - 1)
@@ -466,7 +462,7 @@
             jax.ShapeDtypeStruct(FIELD, f32),
             jax.ShapeDtypeStruct((TABLE, LANES), f32),
         ),
-        in_specs=[VMEM] * 6,
+        in_specs=[VMEM] * 5,
         out_specs=(VMEM,) * 4,
         input_output_aliases={0: 2, 1: 3},
         scratch_shapes=[
@@ -508,21 +504,19 @@
     def ring(count, step):
         return [(i, (i + step) % count) for i in range(count)]
 
-    field, coefs, up_msg, down_msg, left_msg, right_msg = pack(
+    field, coefs, up_msg, down_msg, edge_msg = pack(
         vectors, onsite, intra_hop, inter_index, inter_hop
     )
+    right = lax.ppermute(edge_msg, "col", ring(cols, -1))
+    left = lax.ppermute(edge_msg, "col", ring(cols, 1))
     below = lax.ppermute(up_msg, TILE, ring(tiles, -1))
     above = lax.ppermute(down_msg, TILE, ring(tiles, 1))
-    right = lax.ppermute(left_msg, "col", ring(cols, -1))
-    left = lax.ppermute(right_msg, "col", ring(cols, 1))
     zero, table = own(field, coefs)
-    corner = jnp.concatenate([left, right], axis=0)
-    below_corner = lax.ppermute(corner, TILE, ring(tiles, -1))
-    above_corner = lax.ppermute(corner, TILE, ring(tiles, 1))
+    edge = jnp.where((lanes_of(edge_msg.shape) & 7) < 4, right, left)
+    below_edge = lax.ppermute(edge, TILE, ring(tiles, -1))
+    above_edge = lax.ppermute(edge, TILE, ring(tiles, 1))
     zero, table = near(zero, table, below, above)
-    last_term, partial = apply_terms(
-        devices, zero, table, left, right, below_corner, above_corner
-    )
+    last_term, partial = apply_terms(devices, zero, table, edge, below_edge, above_edge)
     parts = lax.all_to_all(partial, EVERY, 0, 0)
     return last_term, finish(parts, 4.0 * R * C * devices)
 

time: 57.7 us -> 55.3 us (0.958)
  waiting for transfers between devices: 2.47 us -> 7.01 us
  Pallas kernels: 14.7 us -> 10.8 us
  local copies, waits for them, and re-layouts: 2.05 us -> 0 us
  blocking collectives: 24.4 us -> 23.5 us
    ppermute x4, waiting for transfers between devices: 2.46 us -> 7 us  [the longest x1 3.21 us: on_device(): above_edge = lax.ppermute(edge, TILE, ring(tiles, 1))]
    pallas_call x1, Pallas kernels: 10.4 us -> 7.54 us  [apply_terms(): pl.pallas_call(terms_kernel, out_shape=(jax.ShapeDtypeStruct((V, 4, R, C)...]
    unnamed x5 -> x0, local copies, waits for them, and re-layouts: 2.05 us -> none
    pallas_call x1, Pallas kernels: 2.57 us -> 1.45 us  [pack(): pl.pallas_call(pack_kernel, out_shape=(jax.ShapeDtypeStruct((4 * R * V, C...]
    all_to_all x1, blocking collectives: 24.4 us -> 23.5 us  [on_device(): parts = lax.all_to_all(partial, EVERY, 0, 0)]
  transfers between devices with their start and end apart: 6 -> 6, of which waited for: 2 -> 3; matrix products, arithmetic and copies ran while one was open for 0% -> 0% of each run, Pallas kernels for 2% -> 2%
where the time goes in v3:
time: 55.3 us; the launch traced here: 55.2 us
  blocking collectives  23.5 us (42%)
  starting transfers between devices  13.2 us (24%)
  Pallas kernels  10.8 us (20%)
  waiting for transfers between devices  7.01 us (13%)
  between operations  0.68 us (1%)
    all_to_all x1, blocking collectives, on_device(): parts = lax.all_to_all(partial, EVERY, 0, 0)  23.5 us
    pallas_call x1, Pallas kernels, apply_terms(): pl.pallas_call(terms_kernel, out_shape=(jax.ShapeDtypeStruct((V, 4, R, C)...  7.54 us
    ppermute x1, starting transfers between devices, on_device(): below_edge = lax.ppermute(edge, TILE, ring(tiles, -1))  7.31 us
    ppermute x1, starting transfers between devices, on_device(): below = lax.ppermute(up_msg, TILE, ring(tiles, -1))  3.28 us
    ppermute x1, waiting for transfers between devices, on_device(): above_edge = lax.ppermute(edge, TILE, ring(tiles, 1))  3.21 us
    ppermute x1, waiting for transfers between devices, on_device(): left = lax.ppermute(edge_msg, 'col', ring(cols, 1))  2.93 us
    ppermute x1, starting transfers between devices, on_device(): right = lax.ppermute(edge_msg, 'col', ring(cols, -1))  2.64 us
    pallas_call x1, Pallas kernels, pack(): pl.pallas_call(pack_kernel, out_shape=(jax.ShapeDtypeStruct((4 * R * V, C...  1.45 us
  transfers between devices with their start and end apart: 6, of which 3 were waited for; matrix products, arithmetic and copies ran while one was open for 0% of the time, Pallas kernels for 2%

profile of v3, /device:TPU:1, one launch (start us, length us, event | category | flops | bytes accessed | tf_op | source)
XLA Modules:
  0.0 55.2 jit_solution(7195991160164132586)
XLA Ops:
  0.6 1.5 %pack.1 = (f32[256,512]{1,0:T(8,128)S(1)}, f32[208,512]{1,0:T(8,128)S(1)}, f32[200,512]{1,0:T(8,128)S(1)}, f32[200,512]{1,0:T(8,128)S(1)}, f32[32,128]{1,0:T(8,128)S(1)}) custom-call(f32[8,4,8,512]{3,2,1,0:T(8,128)} %vec.1, f32[4,8,512]{2,1,0:T(8,128)} %onsite.1, f32[3,2,8,512]{3,2,1,0:T(8,128)} %intra.1, s32[4,2,8,512]{3,2,1,0:T(8,128)} %codes.1, ...), custom_call_target="tpu_custom_call" | custom-call | tf_op jit(solution)/shard_map/pack/pallas_call | solution.py:121
  2.1 3.3 %collective-permute-start = (f32[200,512]{1,0:T(8,128)S(1)}, f32[200,512]{1,0:T(8,128)S(1)}, u32[]{:S(2)}, u32[]{:S(2)}) collective-permute-start(f32[200,512]{1,0:T(8,128)S(1)} %get-tuple-element.17), channel_id=1, source_target_pairs={{0,63},{1,0},{2,1},{3,2},{4,3},{5,4},{6,5},{7,6},{8,7},{9,8},{10,9... | collective-permute-start | bytes 1228808 | tf_op jit(solution)/shard_map/ppermute | solution.py:512
  5.4 0.0 collective-permute-start.1
  5.4 2.6 %collective-permute-start.2 = (f32[32,128]{1,0:T(8,128)S(1)}, f32[32,128]{1,0:T(8,128)S(1)}, u32[]{:S(2)}, u32[]{:S(2)}) collective-permute-start(f32[32,128]{1,0:T(8,128)S(1)} %get-tuple-element.21), channel_id=1, source_target_pairs={{0,192},{64,0},{128,64},{192,128},{1,193},{65,1},{129,65},{193,129... | collective-permute-start | bytes 49160 | tf_op jit(solution)/shard_map/ppermute | solution.py:510
  8.0 0.0 collective-permute-start.3
  8.0 0.9 %collective-permute-done.2 = f32[32,128]{1,0:T(8,128)S(1)} collective-permute-done((f32[32,128]{1,0:T(8,128)S(1)}, f32[32,128]{1,0:T(8,128)S(1)}, u32[]{:S(2)}, u32[]{:S(2)}) %collective-permute-start.2) | collective-permute-done | bytes 16416 | tf_op jit(solution)/shard_map/ppermute | solution.py:510
  8.9 2.9 %collective-permute-done.3 = f32[32,128]{1,0:T(8,128)S(1)} collective-permute-done((f32[32,128]{1,0:T(8,128)S(1)}, f32[32,128]{1,0:T(8,128)S(1)}, u32[]{:S(2)}, u32[]{:S(2)}) %collective-permute-start.3) | collective-permute-done | bytes 16416 | tf_op jit(solution)/shard_map/ppermute | solution.py:511
  11.8 7.3 %collective-permute-start.4 = (f32[32,128]{1,0:T(8,128)S(1)}, f32[32,128]{1,0:T(8,128)S(1)}, u32[]{:S(2)}, u32[]{:S(2)}) collective-permute-start(f32[32,128]{1,0:T(8,128)S(1)} %broadcast_select_fusion.own_edge), channel_id=1, source_target_pairs={{0,63},{1,0},{2,1},{3,2},{4,3},{5,4},{6,5},{7,6},{8,7},{9,8},{10,9... | collective-permute-start | bytes 49160 | tf_op jit(solution)/shard_map/ppermute | solution.py:516
  19.1 0.0 collective-permute-start.5
  19.1 0.6 own.1
  19.7 0.0 collective-permute-done.below
  19.7 0.0 collective-permute-done.1.above
  19.7 0.5 near.1
  20.2 0.0 collective-permute-done.4.below_edge
  20.2 3.2 %collective-permute-done.5.above_edge = f32[32,128]{1,0:T(8,128)S(1)} collective-permute-done((f32[32,128]{1,0:T(8,128)S(1)}, f32[32,128]{1,0:T(8,128)S(1)}, u32[]{:S(2)}, u32[]{:S(2)}) %collective-permute-start.5) | collective-permute-done | bytes 16416 | tf_op jit(solution)/shard_map/ppermute | solution.py:517
  23.4 7.5 %terms.1 = (f32[8,4,8,512]{3,2,1,0:T(8,128)}, f32[256,128]{1,0:T(8,128)S(1)}, f32[3,544,640]{2,1,0:T(8,128)S(1)}, f32[5840,128]{1,0:T(8,128)S(1)}) custom-call(f32[3,544,640]{2,1,0:T(8,128)S(1)} %get-tuple-element.19.zero_in, f32[5840,128]{1,0:T(8,128)S(1)} %get-tuple-element.20.table_in, ...), custom_call_target="tpu_custom_call", output_to_operand_aliasing={{2}: (0, {}), {3}: (1, {})} | custom-call | tf_op jit(solution)/shard_map/terms/pallas_call | solution.py:457
  31.0 23.5 %all_to_all.11 = f32[256,1,128]{2,1,0:T(1,128)S(1)} all-to-all(f32[256,1,128]{2,1,0:T(1,128)S(1)} %bitcast.5), channel_id=1, replica_groups=mesh['col'=4,'tile_0'=4,'tile_1'=8,'tile_2'=2] {'col','tile_0','tile_1',..., dimensions={0} | all-to-all | bytes 262144 | tf_op jit(solution)/shard_map/all_to_all | solution.py:520
  54.5 0.7 %finish.1 = f32[7,8]{1,0:T(8,128)} custom-call(f32[256,128]{1,0:T(8,128)S(1)} %bitcast.4), custom_call_target="tpu_custom_call" | custom-call | tf_op jit(solution)/shard_map/finish/pallas_call | solution.py:489
  (2 shorter events, 0.0 us)
Async XLA Ops:
  2.1 17.6 %collective-permute-start = (f32[200,512]{1,0:T(8,128)S(1)}, f32[200,512]{1,0:T(8,128)S(1)}, u32[]{:S(2)}, u32[]{:S(2)}) collective-permute-start(f32[200,512]{1,0:T(8,128)S(1)} %get-tuple-element.17), channel_id=1, source_target_pairs={{0,63},{1,0},{2,1},{3,2},{4,3},{5,4},{6,5},{7,6},{8,7},{9,8},{10,9... | collective-permute-start | bytes 1228808 | tf_op jit(solution)/shard_map/ppermute | solution.py:512
  5.4 14.3 %collective-permute-start.1 = (f32[200,512]{1,0:T(8,128)S(1)}, f32[200,512]{1,0:T(8,128)S(1)}, u32[]{:S(2)}, u32[]{:S(2)}) collective-permute-start(f32[200,512]{1,0:T(8,128)S(1)} %get-tuple-element.18), channel_id=1, source_target_pairs={{0,1},{1,2},{2,3},{3,4},{4,5},{5,6},{6,7},{7,8},{8,9},{9,10},{10,1... | collective-permute-start | bytes 1228808 | tf_op jit(solution)/shard_map/ppermute | solution.py:513
  5.4 3.5 %collective-permute-start.2 = (f32[32,128]{1,0:T(8,128)S(1)}, f32[32,128]{1,0:T(8,128)S(1)}, u32[]{:S(2)}, u32[]{:S(2)}) collective-permute-start(f32[32,128]{1,0:T(8,128)S(1)} %get-tuple-element.21), channel_id=1, source_target_pairs={{0,192},{64,0},{128,64},{192,128},{1,193},{65,1},{129,65},{193,129... | collective-permute-start | bytes 49160 | tf_op jit(solution)/shard_map/ppermute | solution.py:510
  8.0 3.8 %collective-permute-start.3 = (f32[32,128]{1,0:T(8,128)S(1)}, f32[32,128]{1,0:T(8,128)S(1)}, u32[]{:S(2)}, u32[]{:S(2)}) collective-permute-start(f32[32,128]{1,0:T(8,128)S(1)} %get-tuple-element.21), channel_id=1, source_target_pairs={{0,64},{64,128},{128,192},{192,0},{1,65},{65,129},{129,193},{193,1... | collective-permute-start | bytes 49160 | tf_op jit(solution)/shard_map/ppermute | solution.py:511
  11.8 8.4 %collective-permute-start.4 = (f32[32,128]{1,0:T(8,128)S(1)}, f32[32,128]{1,0:T(8,128)S(1)}, u32[]{:S(2)}, u32[]{:S(2)}) collective-permute-start(f32[32,128]{1,0:T(8,128)S(1)} %broadcast_select_fusion.own_edge), channel_id=1, source_target_pairs={{0,63},{1,0},{2,1},{3,2},{4,3},{5,4},{6,5},{7,6},{8,7},{9,8},{10,9... | collective-permute-start | bytes 49160 | tf_op jit(solution)/shard_map/ppermute | solution.py:516
  19.1 4.3 %collective-permute-start.5 = (f32[32,128]{1,0:T(8,128)S(1)}, f32[32,128]{1,0:T(8,128)S(1)}, u32[]{:S(2)}, u32[]{:S(2)}) collective-permute-start(f32[32,128]{1,0:T(8,128)S(1)} %broadcast_select_fusion.own_edge), channel_id=1, source_target_pairs={{0,1},{1,2},{2,3},{3,4},{4,5},{5,6},{6,7},{7,8},{8,9},{9,10},{10,1... | collective-permute-start | bytes 49160 | tf_op jit(solution)/shard_map/ppermute | solution.py:517

commit v4 on v3

--- a/solution.py
+++ b/solution.py
@@ -25,7 +25,9 @@
 STEP = RING + 1
 VMEM = pl.BlockSpec(memory_space=pltpu.VMEM)
 FIELD_ROWS = 4 * RIM * V
-ROW_MSG = FIELD_ROWS + COEFS * 4
+TURNED = COEFS // R
+PAIR_ROWS = FIELD_ROWS + TURNED * RIM * R
+ROW_MSG = PAIR_ROWS + (COEFS - TURNED * R) * 4
 
 FWD = 0
 SHIFTED = 36
@@ -90,13 +92,19 @@
     for index in range(COEFS):
         coefs[pl.ds(index * R, R), :] = plane(index)
 
+    for group in range(TURNED):
+        for block in range(BLOCKS):
+            cols = slice(block * LANES, (block + 1) * LANES)
+            values = coefs[pl.ds(group * R * R, R * R), cols].reshape(R, R, LANES)
+            turned = jnp.swapaxes(values, 0, 1)
+            for at in range(RIM):
+                rows = pl.ds(FIELD_ROWS + (group * RIM + at) * R, R)
+                up_msg[rows, cols] = turned[at]
+                down_msg[rows, cols] = turned[R - RIM + at]
     low = subs_of((R, C)) < 4
-    for pair in range(COEFS // 2):
-        even, odd = plane(2 * pair), plane(2 * pair + 1)
-        odd_turned = pltpu.roll(odd, 4, axis=0)
-        rows = pl.ds(FIELD_ROWS + pair * R, R)
-        up_msg[rows, :] = jnp.where(low, even, odd_turned)
-        down_msg[rows, :] = jnp.where(low, odd_turned, even)
+    even, odd = plane(COEFS - 2), pltpu.roll(plane(COEFS - 1), 4, axis=0)
+    up_msg[pl.ds(PAIR_ROWS, R), :] = jnp.where(low, even, odd)
+    down_msg[pl.ds(PAIR_ROWS, R), :] = jnp.where(low, odd, even)
 
     lane = lanes_of((R, LANES))
 
@@ -231,10 +239,21 @@
             put_middle(zero, orbital, R + at, below[rows, :])
             put_middle(zero, orbital, RING - RIM + at, above[rows, :])
     low = subs_of((R, LANES)) < 4
+    turned = {}
+    for group in range(TURNED):
+        for block in range(BLOCKS):
+            cols = slice(block * LANES, (block + 1) * LANES)
+            rows = [pl.ds(FIELD_ROWS + (group * RIM + at) * R, R) for at in range(RIM)]
+            first = [below[at, cols] for at in rows]
+            last = [above[at, cols] for at in rows]
+            values = jnp.stack(first + [first[-1], last[0]] + last)
+            turned[group, block] = jnp.swapaxes(values, 0, 1)
 
     def plane_at(index, block):
+        if index < TURNED * R:
+            return turned[index // R, block][index % R]
         cols = slice(block * LANES, (block + 1) * LANES)
-        rows = pl.ds(FIELD_ROWS + index // 2 * R, R)
+        rows = pl.ds(PAIR_ROWS, R)
         if index % 2 == 0:
             return jnp.where(low, below[rows, cols], above[rows, cols])
         return pltpu.roll(jnp.where(low, above[rows, cols], below[rows, cols]), 4, axis=0)
@@ -294,17 +313,8 @@
                 table[table_rows(shifted, BLOCKS, half), :] = outer
 
 
-def put_rims(zero, table, own_edge, below_edge, above_edge):
-    low = subs_of((R, LANES)) < 4
-    own, below, above = [
-        [ref[8 * at : 8 * at + 8, :] for at in range(4)]
-        for ref in (own_edge, below_edge, above_edge)
-    ]
-    put_field_rims(zero, own[:2], range(R))
-    put_field_rims(zero, below[:2], range(R, R + RIM))
-    put_field_rims(zero, above[:2], range(RING - RIM, RING))
-    put_table_rims(table, own[2:], 0)
-    put_table_rims(table, [jnp.where(low, b, a) for b, a in zip(below[2:], above[2:])], 1)
+def registers(edge):
+    return [edge[8 * at : 8 * at + 8, :] for at in range(4)]
 
 
 def stencil_pair(field, table, row, block):
@@ -391,26 +401,64 @@
     put_down(order[-1])
 
 
+def first_term(zero, one, table, row):
+    term_rows(zero, one, table, row, lambda sums, rows, cols: 0.5 * sums)
+
+
+def second_term(zero, one, two, table, row):
+    term_rows(one, two, table, row, lambda sums, rows, cols: sums - zero[1, rows, cols])
+
+
+def inner_kernel(zero_in, table_in, edge, zero, table, one, two):
+    edges = registers(edge)
+    put_field_rims(zero, edges[:2], range(R))
+    put_table_rims(table, edges[2:], 0)
+
+    def first_rows(step, carry):
+        first_term(zero, one, table, 2 + 2 * step)
+        return carry
+
+    lax.fori_loop(0, 2, first_rows, 0)
+    second_term(zero, one, two, table, 3)
+
+
+def inner(zero, table, edge):
+    f32 = jnp.float32
+    field = jax.ShapeDtypeStruct(FIELD, f32)
+    return pl.pallas_call(
+        inner_kernel,
+        out_shape=(field, jax.ShapeDtypeStruct((TABLE, LANES), f32), field, field),
+        in_specs=[VMEM] * 3,
+        out_specs=(VMEM,) * 4,
+        input_output_aliases={0: 0, 1: 1},
+        compiler_params=pltpu.CompilerParams(vmem_limit_bytes=4 << 20),
+        cost_estimate=pl.CostEstimate(flops=8000000, bytes_accessed=8000000, transcendentals=0),
+        name="inner",
+    )(zero, table, edge)
+
+
 def terms_kernel(
-    zero_in, table_in, own_edge, below_edge, above_edge,
+    zero_in, table_in, one_in, two_in, below_edge, above_edge,
     out, partial, zero, table, one, two, last
 ):
     lane = lanes_of((V, LANES))
-    put_rims(zero, table, own_edge, below_edge, above_edge)
+    low = subs_of((R, LANES)) < 4
+    below, above = registers(below_edge), registers(above_edge)
+    put_field_rims(zero, below[:2], range(R, R + RIM))
+    put_field_rims(zero, above[:2], range(RING - RIM, RING))
+    put_table_rims(table, [jnp.where(low, b, a) for b, a in zip(below[2:], above[2:])], 1)
 
     def first_rows(step, carry):
-        row = (2 * step - 2) & (RING - 1)
-        term_rows(zero, one, table, row, lambda sum_, rows, cols: 0.5 * sum_)
+        first_term(zero, one, table, (2 * step - 2 + 4 * (step >> 1)) & (RING - 1))
         return carry
 
-    lax.fori_loop(0, R // 2 + 2, first_rows, 0)
+    lax.fori_loop(0, 4, first_rows, 0)
 
     def second_rows(step, carry):
-        row = (2 * step - 1) & (RING - 1)
-        term_rows(one, two, table, row, lambda sum_, rows, cols: sum_ - zero[1, rows, cols])
+        second_term(zero, one, two, table, (2 * step - 1 + 2 * (step >> 1)) & (RING - 1))
         return carry
 
-    lax.fori_loop(0, R // 2 + 1, second_rows, 0)
+    lax.fori_loop(0, 4, second_rows, 0)
 
     def third_rows(step, sums):
         row = 2 * step
@@ -461,16 +509,14 @@
             jax.ShapeDtypeStruct((devices, LANES), f32),
             jax.ShapeDtypeStruct(FIELD, f32),
             jax.ShapeDtypeStruct((TABLE, LANES), f32),
+            jax.ShapeDtypeStruct(FIELD, f32),
+            jax.ShapeDtypeStruct(FIELD, f32),
         ),
-        in_specs=[VMEM] * 5,
-        out_specs=(VMEM,) * 4,
-        input_output_aliases={0: 2, 1: 3},
-        scratch_shapes=[
-            pltpu.VMEM(FIELD, f32),
-            pltpu.VMEM(FIELD, f32),
-            pltpu.VMEM((4 * R * V, C), f32),
-        ],
-        compiler_params=pltpu.CompilerParams(vmem_limit_bytes=16 << 20),
+        in_specs=[VMEM] * 6,
+        out_specs=(VMEM,) * 6,
+        input_output_aliases={0: 2, 1: 3, 2: 4, 3: 5},
+        scratch_shapes=[pltpu.VMEM((4 * R * V, C), f32)],
+        compiler_params=pltpu.CompilerParams(vmem_limit_bytes=8 << 20),
         name="terms",
     )(*args)
     return results[0], results[1]
@@ -515,8 +561,11 @@
     edge = jnp.where((lanes_of(edge_msg.shape) & 7) < 4, right, left)
     below_edge = lax.ppermute(edge, TILE, ring(tiles, -1))
     above_edge = lax.ppermute(edge, TILE, ring(tiles, 1))
+    zero, table, one, two = inner(zero, table, edge)
     zero, table = near(zero, table, below, above)
-    last_term, partial = apply_terms(devices, zero, table, edge, below_edge, above_edge)
+    last_term, partial = apply_terms(
+        devices, zero, table, one, two, below_edge, above_edge
+    )
     parts = lax.all_to_all(partial, EVERY, 0, 0)
     return last_term, finish(parts, 4.0 * R * C * devices)
 

time: 55.3 us -> 51.8 us (0.937)
  waiting for transfers between devices: 7.01 us -> 1.13 us
  blocking collectives: 23.5 us -> 25.8 us
    ppermute x1, waiting for transfers between devices: 3.21 us -> 0.01 us  [on_device(): above_edge = lax.ppermute(edge, TILE, ring(tiles, 1))]
    all_to_all x1, blocking collectives: 23.5 us -> 25.8 us  [on_device(): parts = lax.all_to_all(partial, EVERY, 0, 0)]
    ppermute x1, starting transfers between devices: 0.01 us -> 1.83 us  [on_device(): above_edge = lax.ppermute(edge, TILE, ring(tiles, 1))]
    ppermute x1, waiting for transfers between devices: 2.93 us -> 1.12 us  [on_device(): left = lax.ppermute(edge_msg, 'col', ring(cols, 1))]
    ppermute x1, starting transfers between devices: 7.31 us -> 5.54 us  [on_device(): below_edge = lax.ppermute(edge, TILE, ring(tiles, -1))]
    pallas_call x1, Pallas kernels: 7.54 us -> 6.02 us  [apply_terms(): pl.pallas_call(terms_kernel, out_shape=(jax.ShapeDtypeStruct((V, 4, R, C)...]
    pallas_call x0 -> x1, Pallas kernels: none -> 1.51 us  [inner(): pl.pallas_call(inner_kernel, out_shape=(field, jax.ShapeDtypeStruct((TABL...]
    ppermute x1, starting transfers between devices: 0.01 us -> 1.2 us  [on_device(): left = lax.ppermute(edge_msg, 'col', ring(cols, 1))]
  transfers between devices with their start and end apart: 6 -> 6, of which waited for: 3 -> 1; matrix products, arithmetic and copies ran while one was open for 0% -> 0% of each run, Pallas kernels for 2% -> 5%
where the time goes in v4:
time: 51.8 us; the launch traced here: 51.6 us
  blocking collectives  25.8 us (50%)
  starting transfers between devices  13.3 us (26%)
  Pallas kernels  10.7 us (21%)
  waiting for transfers between devices  1.13 us (2%)
  between operations  0.68 us (1%)
    all_to_all x1, blocking collectives, on_device(): parts = lax.all_to_all(partial, EVERY, 0, 0)  25.8 us
    pallas_call x1, Pallas kernels, apply_terms(): pl.pallas_call(terms_kernel, out_shape=(jax.ShapeDtypeStruct((V, 4, R, C)...  6.02 us
    ppermute x1, starting transfers between devices, on_device(): below_edge = lax.ppermute(edge, TILE, ring(tiles, -1))  5.54 us
    ppermute x1, starting transfers between devices, on_device(): below = lax.ppermute(up_msg, TILE, ring(tiles, -1))  3.28 us
    ppermute x1, starting transfers between devices, on_device(): above_edge = lax.ppermute(edge, TILE, ring(tiles, 1))  1.83 us
    pallas_call x1, Pallas kernels, inner(): pl.pallas_call(inner_kernel, out_shape=(field, jax.ShapeDtypeStruct((TABL...  1.51 us
    ppermute x1, starting transfers between devices, on_device(): right = lax.ppermute(edge_msg, 'col', ring(cols, -1))  1.48 us
    pallas_call x1, Pallas kernels, pack(): pl.pallas_call(pack_kernel, out_shape=(jax.ShapeDtypeStruct((4 * R * V, C...  1.45 us
  transfers between devices with their start and end apart: 6, of which 1 were waited for; matrix products, arithmetic and copies ran while one was open for 0% of the time, Pallas kernels for 5%

profile of v4, /device:TPU:1, one launch (start us, length us, event | category | flops | bytes accessed | tf_op | source)
XLA Modules:
  0.0 51.6 jit_solution(16594976239238009950)
XLA Ops:
  0.6 1.5 %pack.1 = (f32[256,512]{1,0:T(8,128)S(1)}, f32[208,512]{1,0:T(8,128)S(1)}, f32[176,512]{1,0:T(8,128)S(1)}, f32[176,512]{1,0:T(8,128)S(1)}, f32[32,128]{1,0:T(8,128)S(1)}) custom-call(f32[8,4,8,512]{3,2,1,0:T(8,128)} %vec.1, f32[4,8,512]{2,1,0:T(8,128)} %onsite.1, f32[3,2,8,512]{3,2,1,0:T(8,128)} %intra.1, s32[4,2,8,512]{3,2,1,0:T(8,128)} %codes.1, ...), custom_call_target="tpu_custom_call" | custom-call | tf_op jit(solution)/shard_map/pack/pallas_call | solution.py:129
  2.1 3.3 %collective-permute-start.2 = (f32[176,512]{1,0:T(8,128)S(1)}, f32[176,512]{1,0:T(8,128)S(1)}, u32[]{:S(2)}, u32[]{:S(2)}) collective-permute-start(f32[176,512]{1,0:T(8,128)S(1)} %get-tuple-element.24), channel_id=1, source_target_pairs={{0,63},{1,0},{2,1},{3,2},{4,3},{5,4},{6,5},{7,6},{8,7},{9,8},{10,9... | collective-permute-start | bytes 1081352 | tf_op jit(solution)/shard_map/ppermute | solution.py:558
  5.4 0.0 collective-permute-start.3
  5.4 1.2 %collective-permute-start.1 = (f32[32,128]{1,0:T(8,128)S(1)}, f32[32,128]{1,0:T(8,128)S(1)}, u32[]{:S(2)}, u32[]{:S(2)}) collective-permute-start(f32[32,128]{1,0:T(8,128)S(1)} %get-tuple-element.21), channel_id=1, source_target_pairs={{0,64},{64,128},{128,192},{192,0},{1,65},{65,129},{129,193},{193,1... | collective-permute-start | bytes 49160 | tf_op jit(solution)/shard_map/ppermute | solution.py:557
  6.6 1.5 %collective-permute-start = (f32[32,128]{1,0:T(8,128)S(1)}, f32[32,128]{1,0:T(8,128)S(1)}, u32[]{:S(2)}, u32[]{:S(2)}) collective-permute-start(f32[32,128]{1,0:T(8,128)S(1)} %get-tuple-element.21), channel_id=1, source_target_pairs={{0,192},{64,0},{128,64},{192,128},{1,193},{65,1},{129,65},{193,129... | collective-permute-start | bytes 49160 | tf_op jit(solution)/shard_map/ppermute | solution.py:556
  8.1 1.1 %collective-permute-done.1 = f32[32,128]{1,0:T(8,128)S(1)} collective-permute-done((f32[32,128]{1,0:T(8,128)S(1)}, f32[32,128]{1,0:T(8,128)S(1)}, u32[]{:S(2)}, u32[]{:S(2)}) %collective-permute-start.1) | collective-permute-done | bytes 16416 | tf_op jit(solution)/shard_map/ppermute | solution.py:557
  9.2 0.0 collective-permute-done
  9.2 1.8 %collective-permute-start.5 = (f32[32,128]{1,0:T(8,128)S(1)}, f32[32,128]{1,0:T(8,128)S(1)}, u32[]{:S(2)}, u32[]{:S(2)}) collective-permute-start(f32[32,128]{1,0:T(8,128)S(1)} %broadcast_select_fusion.edge), channel_id=1, source_target_pairs={{0,1},{1,2},{2,3},{3,4},{4,5},{5,6},{6,7},{7,8},{8,9},{9,10},{10,1... | collective-permute-start | bytes 49160 | tf_op jit(solution)/shard_map/ppermute | solution.py:563
  11.0 5.5 %collective-permute-start.4 = (f32[32,128]{1,0:T(8,128)S(1)}, f32[32,128]{1,0:T(8,128)S(1)}, u32[]{:S(2)}, u32[]{:S(2)}) collective-permute-start(f32[32,128]{1,0:T(8,128)S(1)} %broadcast_select_fusion.edge), channel_id=1, source_target_pairs={{0,63},{1,0},{2,1},{3,2},{4,3},{5,4},{6,5},{7,6},{8,7},{9,8},{10,9... | collective-permute-start | bytes 49160 | tf_op jit(solution)/shard_map/ppermute | solution.py:562
  16.6 0.6 %own.1 = (f32[3,544,640]{2,1,0:T(8,128)S(1)}, f32[5840,128]{1,0:T(8,128)S(1)}) custom-call(f32[256,512]{1,0:T(8,128)S(1)} %get-tuple-element.17.first, f32[208,512]{1,0:T(8,128)S(1)} %get-tuple-element.18.coefs), custom_call_target="tpu_custom_call" | custom-call | flops 4000000 | bytes 4000000 | tf_op jit(solution)/shard_map/own/pallas_call | solution.py:221
  17.1 1.5 %inner.1 = (f32[3,544,640]{2,1,0:T(8,128)S(1)}, f32[5840,128]{1,0:T(8,128)S(1)}, f32[3,544,640]{2,1,0:T(8,128)S(1)}, f32[3,544,640]{2,1,0:T(8,128)S(1)}) custom-call(f32[3,544,640]{2,1,0:T(8,128)S(1)} %get-tuple-element.19.zero_in, f32[5840,128]{1,0:T(8,128)S(1)} %get-tuple-element.20.table_in, ...), custom_call_target="tpu_custom_call", output_to_operand_aliasing={{0}: (0, {}), {1}: (1, {})} | custom-call | flops 8000000 | bytes 8000000 | tf_op jit(solution)/shard_map/inner/pallas_call | solution.py:428
  18.6 0.0 collective-permute-done.2.below
  18.6 0.0 collective-permute-done.3.above
  18.6 0.5 near.1
  19.1 0.0 collective-permute-done.5.above_edge
  19.1 0.0 collective-permute-done.4.below_edge
  19.2 6.0 %terms.1 = (f32[8,4,8,512]{3,2,1,0:T(8,128)}, f32[256,128]{1,0:T(8,128)S(1)}, f32[3,544,640]{2,1,0:T(8,128)S(1)}, f32[5840,128]{1,0:T(8,128)S(1)}, f32[3,544,640...) custom-call(f32[3,544,640]{2,1,0:T(8,128)S(1)} %get-tuple-element.26, ...), custom_call_target="tpu_custom_call", output_to_operand_aliasing={{2}: (0, {}), {3}: (1, {}), {4}: (2, {}), {5}: (3, {})} | custom-call | tf_op jit(solution)/shard_map/terms/pallas_call | solution.py:505
  25.2 25.8 %all_to_all.11 = f32[256,1,128]{2,1,0:T(1,128)S(1)} all-to-all(f32[256,1,128]{2,1,0:T(1,128)S(1)} %bitcast.5), channel_id=1, replica_groups=mesh['col'=4,'tile_0'=4,'tile_1'=8,'tile_2'=2] {'col','tile_0','tile_1',..., dimensions={0} | all-to-all | bytes 262144 | tf_op jit(solution)/shard_map/all_to_all | solution.py:569
  50.9 0.7 %finish.1 = f32[7,8]{1,0:T(8,128)} custom-call(f32[256,128]{1,0:T(8,128)S(1)} %bitcast.4), custom_call_target="tpu_custom_call" | custom-call | tf_op jit(solution)/shard_map/finish/pallas_call | solution.py:535
  (2 shorter events, 0.0 us)
Async XLA Ops:
  2.1 16.5 %collective-permute-start.2 = (f32[176,512]{1,0:T(8,128)S(1)}, f32[176,512]{1,0:T(8,128)S(1)}, u32[]{:S(2)}, u32[]{:S(2)}) collective-permute-start(f32[176,512]{1,0:T(8,128)S(1)} %get-tuple-element.24), channel_id=1, source_target_pairs={{0,63},{1,0},{2,1},{3,2},{4,3},{5,4},{6,5},{7,6},{8,7},{9,8},{10,9... | collective-permute-start | bytes 1081352 | tf_op jit(solution)/shard_map/ppermute | solution.py:558
  5.4 13.3 %collective-permute-start.3 = (f32[176,512]{1,0:T(8,128)S(1)}, f32[176,512]{1,0:T(8,128)S(1)}, u32[]{:S(2)}, u32[]{:S(2)}) collective-permute-start(f32[176,512]{1,0:T(8,128)S(1)} %get-tuple-element.25), channel_id=1, source_target_pairs={{0,1},{1,2},{2,3},{3,4},{4,5},{5,6},{6,7},{7,8},{8,9},{9,10},{10,1... | collective-permute-start | bytes 1081352 | tf_op jit(solution)/shard_map/ppermute | solution.py:559
  5.4 3.8 %collective-permute-start.1 = (f32[32,128]{1,0:T(8,128)S(1)}, f32[32,128]{1,0:T(8,128)S(1)}, u32[]{:S(2)}, u32[]{:S(2)}) collective-permute-start(f32[32,128]{1,0:T(8,128)S(1)} %get-tuple-element.21), channel_id=1, source_target_pairs={{0,64},{64,128},{128,192},{192,0},{1,65},{65,129},{129,193},{193,1... | collective-permute-start | bytes 49160 | tf_op jit(solution)/shard_map/ppermute | solution.py:557
  6.6 2.6 %collective-permute-start = (f32[32,128]{1,0:T(8,128)S(1)}, f32[32,128]{1,0:T(8,128)S(1)}, u32[]{:S(2)}, u32[]{:S(2)}) collective-permute-start(f32[32,128]{1,0:T(8,128)S(1)} %get-tuple-element.21), channel_id=1, source_target_pairs={{0,192},{64,0},{128,64},{192,128},{1,193},{65,1},{129,65},{193,129... | collective-permute-start | bytes 49160 | tf_op jit(solution)/shard_map/ppermute | solution.py:556
  9.2 10.0 %collective-permute-start.5 = (f32[32,128]{1,0:T(8,128)S(1)}, f32[32,128]{1,0:T(8,128)S(1)}, u32[]{:S(2)}, u32[]{:S(2)}) collective-permute-start(f32[32,128]{1,0:T(8,128)S(1)} %broadcast_select_fusion.edge), channel_id=1, source_target_pairs={{0,1},{1,2},{2,3},{3,4},{4,5},{5,6},{6,7},{7,8},{8,9},{9,10},{10,1... | collective-permute-start | bytes 49160 | tf_op jit(solution)/shard_map/ppermute | solution.py:563
  11.0 8.1 %collective-permute-start.4 = (f32[32,128]{1,0:T(8,128)S(1)}, f32[32,128]{1,0:T(8,128)S(1)}, u32[]{:S(2)}, u32[]{:S(2)}) collective-permute-start(f32[32,128]{1,0:T(8,128)S(1)} %broadcast_select_fusion.edge), channel_id=1, source_target_pairs={{0,63},{1,0},{2,1},{3,2},{4,3},{5,4},{6,5},{7,6},{8,7},{9,8},{10,9... | collective-permute-start | bytes 49160 | tf_op jit(solution)/shard_map/ppermute | solution.py:562

commit v5 on v4

--- a/solution.py
+++ b/solution.py
@@ -187,10 +187,7 @@
 
 
 def field_rows(orbital, row):
-    start = (orbital * STEP + row) * V
-    if not isinstance(start, int):
-        start = pl.multiple_of(start, V)
-    return pl.ds(start, V)
+    return pl.ds((orbital * STEP + row % RING) * V, V)
 
 
 def put_middle(field, orbital, row, values):
@@ -317,23 +314,25 @@
     return [edge[8 * at : 8 * at + 8, :] for at in range(4)]
 
 
-def stencil_pair(field, table, row, block):
+def stencil_pair(field, table, pair, block):
     cols = slice(block * LANES, (block + 1) * LANES)
-    at = {step: (row + step) & (RING - 1) for step in range(-1, 3)}
-    start = {step: (block * RING + at[step]) * STRIDE for step in at}
+
+    def start(row):
+        return (block * RING + row % RING) * STRIDE
+
     sums = [[None] * 4 for _ in range(2)]
 
-    def add(cell, orbital, plane, step, value):
-        coef = table[pl.ds(start[step] + plane, V, stride=0), :]
+    def add(cell, orbital, plane, row, value):
+        coef = table[pl.ds(start(row) + plane, V, stride=0), :]
         term = coef * value
         old = sums[cell][orbital]
         sums[cell][orbital] = term if old is None else old + term
 
-    for step in range(-1, 3):
+    for there in sorted({row + step for row in pair for step in (-1, 0, 1)}):
         for col_off in (-1, 0, 1):
-            value = [field[1 + col_off, field_rows(o, at[step]), cols] for o in range(4)]
-            for cell in range(2):
-                row_off = step - cell
+            value = [field[1 + col_off, field_rows(o, there), cols] for o in range(4)]
+            for cell, here in enumerate(pair):
+                row_off = there - here
                 if abs(row_off) > 1:
                     continue
                 code = (row_off + 1) * 3 + col_off + 1
@@ -341,32 +340,32 @@
                 for source in range(2):
                     for target in range(2):
                         plane = FWD + source * 18 + 9 * target + code
-                        add(cell, source, plane, cell, value[2 + target])
+                        add(cell, source, plane, here, value[2 + target])
                         plane = shifted_plane(source, 9 * target + back)
-                        add(cell, 2 + target, plane, step, value[source])
+                        add(cell, 2 + target, plane, there, value[source])
                 for layer in range(2):
                     a, b = 2 * layer, 2 * layer + 1
                     if (row_off, col_off) == (0, 0):
-                        add(cell, a, ONSITE + a, cell, value[a])
-                        add(cell, b, ONSITE + b, cell, value[b])
-                        add(cell, a, INTRA + layer, cell, value[b])
-                        add(cell, b, INTRA + layer, cell, value[a])
+                        add(cell, a, ONSITE + a, here, value[a])
+                        add(cell, b, ONSITE + b, here, value[b])
+                        add(cell, a, INTRA + layer, here, value[b])
+                        add(cell, b, INTRA + layer, here, value[a])
                     elif (row_off, col_off) == (-1, 0):
-                        add(cell, a, INTRA + 2 + layer, cell, value[b])
+                        add(cell, a, INTRA + 2 + layer, here, value[b])
                     elif (row_off, col_off) == (1, 0):
-                        add(cell, b, INTRA + 2 + layer, step, value[a])
+                        add(cell, b, INTRA + 2 + layer, there, value[a])
                     elif (row_off, col_off) == (0, -1):
-                        add(cell, a, INTRA + 4 + layer, cell, value[b])
+                        add(cell, a, INTRA + 4 + layer, here, value[b])
                     elif (row_off, col_off) == (0, 1):
-                        add(cell, b, INTRA_SHIFTED + layer, cell, value[a])
+                        add(cell, b, INTRA_SHIFTED + layer, here, value[a])
     return sums
 
 
-def term_rows(source, target, table, row, value_of):
+def term_rows(source, target, table, pair, value_of):
     lane = lanes_of((V, LANES))
     count = BLOCKS + 1
     keys = [(cell, orbital) for cell in range(2) for orbital in range(4)]
-    rows = {key: field_rows(key[1], (row + key[0]) & (RING - 1)) for key in keys}
+    rows = {key: field_rows(key[1], pair[key[0]]) for key in keys}
     up, down = {}, {}
 
     def columns(block):
@@ -388,7 +387,7 @@
 
     order = [BLOCKS] + list(range(BLOCKS))
     for at, block in enumerate(order):
-        result = stencil_pair(source, table, row, block)
+        result = stencil_pair(source, table, pair, block)
         for key in keys:
             value = value_of(result[key[0]][key[1]], rows[key], columns(block))
             target[1, rows[key], columns(block)] = value
@@ -401,12 +400,12 @@
     put_down(order[-1])
 
 
-def first_term(zero, one, table, row):
-    term_rows(zero, one, table, row, lambda sums, rows, cols: 0.5 * sums)
-
-
-def second_term(zero, one, two, table, row):
-    term_rows(one, two, table, row, lambda sums, rows, cols: sums - zero[1, rows, cols])
+def first_term(zero, one, table, pair):
+    term_rows(zero, one, table, pair, lambda sums, rows, cols: 0.5 * sums)
+
+
+def second_term(zero, one, two, table, pair):
+    term_rows(one, two, table, pair, lambda sums, rows, cols: sums - zero[1, rows, cols])
 
 
 def inner_kernel(zero_in, table_in, edge, zero, table, one, two):
@@ -414,12 +413,10 @@
     put_field_rims(zero, edges[:2], range(R))
     put_table_rims(table, edges[2:], 0)
 
-    def first_rows(step, carry):
-        first_term(zero, one, table, 2 + 2 * step)
-        return carry
-
-    lax.fori_loop(0, 2, first_rows, 0)
-    second_term(zero, one, two, table, 3)
+    for pair in ((1, 2), (3, 4), (5, 6)):
+        first_term(zero, one, table, pair)
+    for pair in ((2, 3), (4, 5)):
+        second_term(zero, one, two, table, pair)
 
 
 def inner(zero, table, edge):
@@ -439,7 +436,7 @@
 
 def terms_kernel(
     zero_in, table_in, one_in, two_in, below_edge, above_edge,
-    out, partial, zero, table, one, two, last
+    out, partial, zero, table, one, two, last, turned, sems
 ):
     lane = lanes_of((V, LANES))
     low = subs_of((R, LANES)) < 4
@@ -448,48 +445,41 @@
     put_field_rims(zero, above[:2], range(RING - RIM, RING))
     put_table_rims(table, [jnp.where(low, b, a) for b, a in zip(below[2:], above[2:])], 1)
 
-    def first_rows(step, carry):
-        first_term(zero, one, table, (2 * step - 2 + 4 * (step >> 1)) & (RING - 1))
-        return carry
-
-    lax.fori_loop(0, 4, first_rows, 0)
-
-    def second_rows(step, carry):
-        second_term(zero, one, two, table, (2 * step - 1 + 2 * (step >> 1)) & (RING - 1))
-        return carry
-
-    lax.fori_loop(0, 4, second_rows, 0)
-
-    def third_rows(step, sums):
-        row = 2 * step
-        sums = list(sums)
-        for block in range(BLOCKS):
-            cols = slice(block * LANES, (block + 1) * LANES)
-            result = stencil_pair(two, table, row, block)
-            for cell in range(2):
+    for pair in ((-2, -1), (0, 7), (8, 9)):
+        first_term(zero, one, table, pair)
+    for pair in ((-1, 0), (1, 6), (7, 8)):
+        second_term(zero, one, two, table, pair)
+
+    empty = jnp.zeros((V, LANES), jnp.float32)
+    sums = [empty] * 7
+    copies = []
+    for block in range(BLOCKS):
+        cols = slice(block * LANES, (block + 1) * LANES)
+        for pair in ((0, 1), (2, 3), (4, 5), (6, 7)):
+            result = stencil_pair(two, table, pair, block)
+            for cell, row in enumerate(pair):
                 for orbital in range(4):
-                    rows = field_rows(orbital, row + cell)
+                    rows = field_rows(orbital, row)
                     t0 = zero[1, rows, cols]
                     t1 = one[1, rows, cols]
                     t2 = two[1, rows, cols]
                     t3 = result[cell][orbital] - t1
-                    at = pl.multiple_of((orbital * R + row + cell) * V, V)
-                    last[pl.ds(at, V), cols] = t3
+                    last[pl.ds((orbital * R + row) * V, V), cols] = t3
                     for at, (x, y) in enumerate(
                         ((t0, t0), (t1, t0), (t1, t1), (t2, t1), (t2, t2), (t3, t2), (t3, t3))
                     ):
                         sums[at] = sums[at] + x * y
-        return tuple(sums)
-
-    empty = jnp.zeros((V, LANES), jnp.float32)
-    sums = lax.fori_loop(0, R // 2, third_rows, (empty,) * 7)
-
-    for orbital in range(4):
-        for block in range(BLOCKS):
-            cols = slice(block * LANES, (block + 1) * LANES)
+        for orbital in range(4):
             rows = pl.ds(orbital * R * V, R * V)
-            turned = jnp.swapaxes(last[rows, cols].reshape(R, V, LANES), 0, 1)
-            out[:, orbital, :, cols] = turned
+            values = last[rows, cols].reshape(R, V, LANES)
+            turned[:, orbital, :, cols] = jnp.swapaxes(values, 0, 1)
+        copies.append(
+            pltpu.make_async_copy(
+                turned.at[:, :, :, cols], out.at[:, :, :, cols], sems.at[block]
+            )
+        )
+        if block > 0:
+            copies[block - 1].start()
 
     spread = empty
     sub = subs_of((V, LANES))
@@ -498,6 +488,9 @@
         spread = jnp.where(lane == 8 * at + sub, total, spread)
     line = jnp.sum(spread, axis=0, keepdims=True)
     partial[...] = jnp.broadcast_to(line, partial.shape)
+    copies[-1].start()
+    for copy in copies:
+        copy.wait()
 
 
 def apply_terms(devices, *args):
@@ -513,9 +506,13 @@
             jax.ShapeDtypeStruct(FIELD, f32),
         ),
         in_specs=[VMEM] * 6,
-        out_specs=(VMEM,) * 6,
+        out_specs=(pl.BlockSpec(memory_space=pltpu.HBM),) + (VMEM,) * 5,
         input_output_aliases={0: 2, 1: 3, 2: 4, 3: 5},
-        scratch_shapes=[pltpu.VMEM((4 * R * V, C), f32)],
+        scratch_shapes=[
+            pltpu.VMEM((4 * R * V, C), f32),
+            pltpu.VMEM((V, 4, R, C), f32),
+            pltpu.SemaphoreType.DMA((BLOCKS,)),
+        ],
         compiler_params=pltpu.CompilerParams(vmem_limit_bytes=8 << 20),
         name="terms",
     )(*args)

time: 51.8 us -> 50.1 us (0.967)
  Pallas kernels: 10.7 us -> 9.4 us
    pallas_call x1, Pallas kernels: 6.02 us -> 4.35 us  [apply_terms(): pl.pallas_call(terms_kernel, out_shape=(jax.ShapeDtypeStruct((V, 4, R, C)...]
  transfers between devices with their start and end apart: 6 -> 6, of which waited for: 1 -> 1; matrix products, arithmetic and copies ran while one was open for 0% -> 0% of each run, Pallas kernels for 5% -> 6%
where the time goes in v5:
time: 50.1 us; the launch traced here: 50 us
  blocking collectives  25.4 us (51%)
  starting transfers between devices  13.3 us (27%)
  Pallas kernels  9.4 us (19%)
  waiting for transfers between devices  1.13 us (2%)
  between operations  0.7 us (1%)
    all_to_all x1, blocking collectives, on_device(): parts = lax.all_to_all(partial, EVERY, 0, 0)  25.4 us
    ppermute x1, starting transfers between devices, on_device(): below_edge = lax.ppermute(edge, TILE, ring(tiles, -1))  5.54 us
    pallas_call x1, Pallas kernels, apply_terms(): pl.pallas_call(terms_kernel, out_shape=(jax.ShapeDtypeStruct((V, 4, R, C)...  4.35 us
    ppermute x1, starting transfers between devices, on_device(): below = lax.ppermute(up_msg, TILE, ring(tiles, -1))  3.28 us
    pallas_call x1, Pallas kernels, inner(): pl.pallas_call(inner_kernel, out_shape=(field, jax.ShapeDtypeStruct((TABL...  1.84 us
    ppermute x1, starting transfers between devices, on_device(): above_edge = lax.ppermute(edge, TILE, ring(tiles, 1))  1.83 us
    ppermute x1, starting transfers between devices, on_device(): right = lax.ppermute(edge_msg, 'col', ring(cols, -1))  1.48 us
    pallas_call x1, Pallas kernels, pack(): pl.pallas_call(pack_kernel, out_shape=(jax.ShapeDtypeStruct((4 * R * V, C...  1.45 us
  transfers between devices with their start and end apart: 6, of which 1 were waited for; matrix products, arithmetic and copies ran while one was open for 0% of the time, Pallas kernels for 6%

profile of v5, /device:TPU:1, one launch (start us, length us, event | category | flops | bytes accessed | tf_op | source)
XLA Modules:
  0.0 50.0 jit_solution(17245939163654876226)
XLA Ops:
  0.6 1.5 %pack.1 = (f32[256,512]{1,0:T(8,128)S(1)}, f32[208,512]{1,0:T(8,128)S(1)}, f32[176,512]{1,0:T(8,128)S(1)}, f32[176,512]{1,0:T(8,128)S(1)}, f32[32,128]{1,0:T(8,128)S(1)}) custom-call(f32[8,4,8,512]{3,2,1,0:T(8,128)} %vec.1, f32[4,8,512]{2,1,0:T(8,128)} %onsite.1, f32[3,2,8,512]{3,2,1,0:T(8,128)} %intra.1, s32[4,2,8,512]{3,2,1,0:T(8,128)} %codes.1, ...), custom_call_target="tpu_custom_call" | custom-call | tf_op jit(solution)/shard_map/pack/pallas_call | solution.py:129
  2.1 3.3 %collective-permute-start.2 = (f32[176,512]{1,0:T(8,128)S(1)}, f32[176,512]{1,0:T(8,128)S(1)}, u32[]{:S(2)}, u32[]{:S(2)}) collective-permute-start(f32[176,512]{1,0:T(8,128)S(1)} %get-tuple-element.24), channel_id=1, source_target_pairs={{0,63},{1,0},{2,1},{3,2},{4,3},{5,4},{6,5},{7,6},{8,7},{9,8},{10,9... | collective-permute-start | bytes 1081352 | tf_op jit(solution)/shard_map/ppermute | solution.py:555
  5.4 0.0 collective-permute-start.3
  5.4 1.2 %collective-permute-start.1 = (f32[32,128]{1,0:T(8,128)S(1)}, f32[32,128]{1,0:T(8,128)S(1)}, u32[]{:S(2)}, u32[]{:S(2)}) collective-permute-start(f32[32,128]{1,0:T(8,128)S(1)} %get-tuple-element.21), channel_id=1, source_target_pairs={{0,64},{64,128},{128,192},{192,0},{1,65},{65,129},{129,193},{193,1... | collective-permute-start | bytes 49160 | tf_op jit(solution)/shard_map/ppermute | solution.py:554
  6.6 1.5 %collective-permute-start = (f32[32,128]{1,0:T(8,128)S(1)}, f32[32,128]{1,0:T(8,128)S(1)}, u32[]{:S(2)}, u32[]{:S(2)}) collective-permute-start(f32[32,128]{1,0:T(8,128)S(1)} %get-tuple-element.21), channel_id=1, source_target_pairs={{0,192},{64,0},{128,64},{192,128},{1,193},{65,1},{129,65},{193,129... | collective-permute-start | bytes 49160 | tf_op jit(solution)/shard_map/ppermute | solution.py:553
  8.1 1.1 %collective-permute-done.1 = f32[32,128]{1,0:T(8,128)S(1)} collective-permute-done((f32[32,128]{1,0:T(8,128)S(1)}, f32[32,128]{1,0:T(8,128)S(1)}, u32[]{:S(2)}, u32[]{:S(2)}) %collective-permute-start.1) | collective-permute-done | bytes 16416 | tf_op jit(solution)/shard_map/ppermute | solution.py:554
  9.2 0.0 collective-permute-done
  9.2 1.8 %collective-permute-start.5 = (f32[32,128]{1,0:T(8,128)S(1)}, f32[32,128]{1,0:T(8,128)S(1)}, u32[]{:S(2)}, u32[]{:S(2)}) collective-permute-start(f32[32,128]{1,0:T(8,128)S(1)} %broadcast_select_fusion.edge), channel_id=1, source_target_pairs={{0,1},{1,2},{2,3},{3,4},{4,5},{5,6},{6,7},{7,8},{8,9},{9,10},{10,1... | collective-permute-start | bytes 49160 | tf_op jit(solution)/shard_map/ppermute | solution.py:560
  11.0 5.5 %collective-permute-start.4 = (f32[32,128]{1,0:T(8,128)S(1)}, f32[32,128]{1,0:T(8,128)S(1)}, u32[]{:S(2)}, u32[]{:S(2)}) collective-permute-start(f32[32,128]{1,0:T(8,128)S(1)} %broadcast_select_fusion.edge), channel_id=1, source_target_pairs={{0,63},{1,0},{2,1},{3,2},{4,3},{5,4},{6,5},{7,6},{8,7},{9,8},{10,9... | collective-permute-start | bytes 49160 | tf_op jit(solution)/shard_map/ppermute | solution.py:559
  16.6 0.6 %own.1 = (f32[3,544,640]{2,1,0:T(8,128)S(1)}, f32[5840,128]{1,0:T(8,128)S(1)}) custom-call(f32[256,512]{1,0:T(8,128)S(1)} %get-tuple-element.17.first, f32[208,512]{1,0:T(8,128)S(1)} %get-tuple-element.18.coefs), custom_call_target="tpu_custom_call" | custom-call | flops 4000000 | bytes 4000000 | tf_op jit(solution)/shard_map/own/pallas_call | solution.py:218
  17.1 1.8 %inner.1 = (f32[3,544,640]{2,1,0:T(8,128)S(1)}, f32[5840,128]{1,0:T(8,128)S(1)}, f32[3,544,640]{2,1,0:T(8,128)S(1)}, f32[3,544,640]{2,1,0:T(8,128)S(1)}) custom-call(f32[3,544,640]{2,1,0:T(8,128)S(1)} %get-tuple-element.19.zero_in, f32[5840,128]{1,0:T(8,128)S(1)} %get-tuple-element.20.table_in, ...), custom_call_target="tpu_custom_call", output_to_operand_aliasing={{0}: (0, {}), {1}: (1, {})} | custom-call | flops 8000000 | bytes 8000000 | tf_op jit(solution)/shard_map/inner/pallas_call | solution.py:425
  19.0 0.0 collective-permute-done.2.below
  19.0 0.0 collective-permute-done.3.above
  19.0 0.5 near.1
  19.5 0.0 collective-permute-done.5.above_edge
  19.5 0.0 collective-permute-done.4.below_edge
  19.5 4.4 %terms.1 = (f32[8,4,8,512]{3,2,1,0:T(8,128)}, f32[256,128]{1,0:T(8,128)S(1)}, f32[3,544,640]{2,1,0:T(8,128)S(1)}, f32[5840,128]{1,0:T(8,128)S(1)}, f32[3,544,640...) custom-call(f32[3,544,640]{2,1,0:T(8,128)S(1)} %get-tuple-element.26, ...), custom_call_target="tpu_custom_call", output_to_operand_aliasing={{2}: (0, {}), {3}: (1, {}), {4}: (2, {}), {5}: (3, {})} | custom-call | tf_op jit(solution)/shard_map/terms/pallas_call | solution.py:498
  23.9 25.4 %all_to_all.11 = f32[256,1,128]{2,1,0:T(1,128)S(1)} all-to-all(f32[256,1,128]{2,1,0:T(1,128)S(1)} %bitcast.5), channel_id=1, replica_groups=mesh['col'=4,'tile_0'=4,'tile_1'=8,'tile_2'=2] {'col','tile_0','tile_1',..., dimensions={0} | all-to-all | bytes 262144 | tf_op jit(solution)/shard_map/all_to_all | solution.py:566
  49.3 0.7 %finish.1 = f32[7,8]{1,0:T(8,128)} custom-call(f32[256,128]{1,0:T(8,128)S(1)} %bitcast.4), custom_call_target="tpu_custom_call" | custom-call | tf_op jit(solution)/shard_map/finish/pallas_call | solution.py:532
  (2 shorter events, 0.0 us)
Async XLA Ops:
  2.1 16.9 %collective-permute-start.2 = (f32[176,512]{1,0:T(8,128)S(1)}, f32[176,512]{1,0:T(8,128)S(1)}, u32[]{:S(2)}, u32[]{:S(2)}) collective-permute-start(f32[176,512]{1,0:T(8,128)S(1)} %get-tuple-element.24), channel_id=1, source_target_pairs={{0,63},{1,0},{2,1},{3,2},{4,3},{5,4},{6,5},{7,6},{8,7},{9,8},{10,9... | collective-permute-start | bytes 1081352 | tf_op jit(solution)/shard_map/ppermute | solution.py:555
  5.4 13.6 %collective-permute-start.3 = (f32[176,512]{1,0:T(8,128)S(1)}, f32[176,512]{1,0:T(8,128)S(1)}, u32[]{:S(2)}, u32[]{:S(2)}) collective-permute-start(f32[176,512]{1,0:T(8,128)S(1)} %get-tuple-element.25), channel_id=1, source_target_pairs={{0,1},{1,2},{2,3},{3,4},{4,5},{5,6},{6,7},{7,8},{8,9},{9,10},{10,1... | collective-permute-start | bytes 1081352 | tf_op jit(solution)/shard_map/ppermute | solution.py:556
  5.4 3.8 %collective-permute-start.1 = (f32[32,128]{1,0:T(8,128)S(1)}, f32[32,128]{1,0:T(8,128)S(1)}, u32[]{:S(2)}, u32[]{:S(2)}) collective-permute-start(f32[32,128]{1,0:T(8,128)S(1)} %get-tuple-element.21), channel_id=1, source_target_pairs={{0,64},{64,128},{128,192},{192,0},{1,65},{65,129},{129,193},{193,1... | collective-permute-start | bytes 49160 | tf_op jit(solution)/shard_map/ppermute | solution.py:554
  6.6 2.6 %collective-permute-start = (f32[32,128]{1,0:T(8,128)S(1)}, f32[32,128]{1,0:T(8,128)S(1)}, u32[]{:S(2)}, u32[]{:S(2)}) collective-permute-start(f32[32,128]{1,0:T(8,128)S(1)} %get-tuple-element.21), channel_id=1, source_target_pairs={{0,192},{64,0},{128,64},{192,128},{1,193},{65,1},{129,65},{193,129... | collective-permute-start | bytes 49160 | tf_op jit(solution)/shard_map/ppermute | solution.py:553
  9.2 10.3 %collective-permute-start.5 = (f32[32,128]{1,0:T(8,128)S(1)}, f32[32,128]{1,0:T(8,128)S(1)}, u32[]{:S(2)}, u32[]{:S(2)}) collective-permute-start(f32[32,128]{1,0:T(8,128)S(1)} %broadcast_select_fusion.edge), channel_id=1, source_target_pairs={{0,1},{1,2},{2,3},{3,4},{4,5},{5,6},{6,7},{7,8},{8,9},{9,10},{10,1... | collective-permute-start | bytes 49160 | tf_op jit(solution)/shard_map/ppermute | solution.py:560
  11.0 8.5 %collective-permute-start.4 = (f32[32,128]{1,0:T(8,128)S(1)}, f32[32,128]{1,0:T(8,128)S(1)}, u32[]{:S(2)}, u32[]{:S(2)}) collective-permute-start(f32[32,128]{1,0:T(8,128)S(1)} %broadcast_select_fusion.edge), channel_id=1, source_target_pairs={{0,63},{1,0},{2,1},{3,2},{4,3},{5,4},{6,5},{7,6},{8,7},{9,8},{10,9... | collective-permute-start | bytes 49160 | tf_op jit(solution)/shard_map/ppermute | solution.py:559
